TPU v7x, 512 devices: a 8x2x16 block of a 8x16x16 slice. The times are simulated.
512 devices in a mesh: parts: 2 (over y), space: 16 (over z), tm: 8 (over x), chan: 2 (over core).
Axes of the slice: x: 8, y: 2, z: 16, core: 2. Of those that a mesh axis runs over, the one named last changes fastest.
The devices are a block of a 8x16x16 slice.
Arguments:
- events: int32 [64, 128, 128], P(('parts', 'tm'), 'space'), parts along dimension 0, may hold values 0 or 1
- soft_info: bfloat16 [64, 128, 128], P(('parts', 'tm'), 'space'), parts along dimension 0, may hold values from -6 to 6
- embed: float32 [4, 64], replicated, may hold values from -6 to 6
- soft_gain: float32 [64], replicated, may hold values from -6 to 6
- conv_weights: bfloat16 [3, 64, 1728], replicated, may hold values from -0.21875 to 0.21875
- conv_bias: float32 [3, 64], replicated, may hold values from -1.75 to 1.75
- readout_weight: float32 [64], replicated, may hold values from -0.75 to 0.75
Outputs:
- logits: float32 [64, 128, 128], P(('parts', 'tm'), 'space'), parts along dimension 0
There are 2 independent parts, one for each index of `parts`. A program takes and returns all parts, laid end to end along the dimension named above; an argument that names none is the same for every part. Nothing has to cross between parts.
All inputs are finite; a program needn't handle non-finite values. No bound on the sum of `events` on one device may be relied on, other than what follows from the above.
Results may differ from a plain program's by a relative error of at most 0.024.
Values may be sent and summed in bfloat16 or wider, within the bound.
A program may use at most 64 MiB of HBM per device.

v0:
```python
import jax
import jax.numpy as jnp
from jax import lax
from jax.sharding import PartitionSpec as P


def with_halo(value, sides, width):
    edges = {}
    for axis, dim in sides:
        peers, length = (lax.axis_size(axis), value.shape[dim])
        up = [(i, (i + 1) % peers) for i in range(peers - 1)]
        last = lax.slice_in_dim(value, length - width, length, axis=dim)
        first = lax.slice_in_dim(value, 0, width, axis=dim)
        edges[dim] = (
            lax.ppermute(last, axis, up),
            lax.ppermute(first, axis, [(b, a) for a, b in up]),
        )
    done = []
    for _, dim in sides:
        low, high = edges[dim]
        around = [(width, width) if d in done else (0, 0) for d in range(value.ndim)]
        value = jnp.concatenate([jnp.pad(low, around), value, jnp.pad(high, around)], axis=dim)
        done.append(dim)
    return value


def from_behind(value, axis, by):
    peers = lax.axis_size(axis)
    pairs = [(i, i + by) for i in range(peers) if 0 <= i + by < peers]
    return lax.ppermute(value, axis, pairs)


def from_everyone(value, axis):
    copies = jnp.broadcast_to(value, (lax.axis_size(axis), *value.shape))
    return lax.all_to_all(copies, axis, split_axis=0, concat_axis=0, tiled=True)


def in_order(pieces, dim):
    dims = list(pieces.shape[1:])
    dims[dim] *= pieces.shape[0]
    return jnp.moveaxis(pieces, 0, dim).reshape(dims)


def gather_directly(value, axis, dim):
    pieces = from_everyone(value, axis)
    return in_order(pieces, dim)


def correlate(inputs, kernel):
    output = lax.conv_general_dilated(
        inputs[None],
        kernel,
        (1, 1, 1),
        ((0, 0), (0, 0), (1, 1)),
        dimension_numbers=("NCDHW", "OIDHW", "NCDHW"),
        preferred_element_type=jnp.float32,
    )
    return output[0]


def widen(features, depth):
    return with_halo(features, ((("space", "chan"), 2),), depth)


def widen_inputs(stacked, depth):
    return with_halo(stacked, ((("space", "chan"), 2),), depth)


def per_device(events, soft_info, embed, soft_gain, conv_weights, conv_bias, readout_weight):
    half_rounds = events.shape[0] // 2
    tile_rows = events.shape[1]
    columns = events.shape[2]
    grid_rows = tile_rows * lax.axis_size("space")
    pair_size = lax.axis_size("chan")
    layers = conv_weights.shape[0]
    channels = embed.shape[1]
    space_pos = lax.axis_index("space")
    chan_pos = lax.axis_index("chan")
    strip = tile_rows // pair_size
    events = lax.dynamic_slice_in_dim(events, chan_pos * strip, strip, 1)
    soft_info = lax.dynamic_slice_in_dim(soft_info, chan_pos * strip, strip, 1)
    row_start = (space_pos * pair_size + chan_pos) * strip
    stacked = jnp.stack([events.astype(jnp.bfloat16), soft_info], 0)
    stacked = widen_inputs(stacked, layers)
    events = stacked[0].astype(jnp.int32)
    soft_info = stacked[1]
    first_row = row_start - layers
    made_rows = events.shape[1]
    row_index = first_row + jnp.arange(made_rows, dtype=jnp.int32)
    col_index = jnp.arange(columns, dtype=jnp.int32)
    parity = (row_index[:, None] + col_index[None, :]) % 2
    code = 2 * parity[None] + events
    onehot = (code[None] == jnp.arange(4, dtype=jnp.int32)[:, None, None, None]).astype(jnp.float32)
    start = (
        jnp.einsum("kc,kryx->cryx", embed, onehot)
        + soft_gain[:, None, None, None] * soft_info.astype(jnp.float32)[None]
    )
    start = start.astype(jnp.bfloat16)
    within = (row_index >= 0) & (row_index < grid_rows)
    start = jnp.where(within[None, None, :, None], start, jnp.zeros((), jnp.bfloat16))
    kernels = conv_weights.reshape(layers, channels, channels, 3, 3, 3)

    def apply_layer(padded, layer):
        summed = correlate(padded, kernels[layer])
        return jnp.maximum(summed + conv_bias[layer][:, None, None, None], 0.0).astype(jnp.bfloat16)

    def run_wide(hidden, front_wide, back_wide):
        for layer in range(layers):
            span = hidden.shape[2]
            joined = jnp.concatenate(
                [
                    front_wide[:, :, layer : layer + span],
                    hidden,
                    back_wide[:, :, layer : layer + span],
                ],
                1,
            )
            hidden = apply_layer(joined, layer)
            margin = layers - layer - 1
            if margin > 0:
                global_rows = row_start - margin + jnp.arange(hidden.shape[2], dtype=jnp.int32)
                inside = (global_rows >= 0) & (global_rows < grid_rows)
                hidden = jnp.where(inside[None, None, :, None], hidden, jnp.zeros((), jnp.bfloat16))
        return hidden

    blank_wide = jnp.zeros((channels, 1, made_rows, columns), jnp.bfloat16)
    first = run_wide(start[:, :half_rounds], blank_wide, blank_wide)
    following = from_behind(first[:, :1], "tm", -1)
    slabs = widen(jnp.concatenate([first[:, -1:], following], 1), layers)
    second = run_wide(start[:, half_rounds:], slabs[:, :1], slabs[:, 1:])
    final = jnp.concatenate([first, second], 1)
    partial_value = jnp.einsum("c,cryx->ryx", readout_weight, final.astype(jnp.float32))
    return gather_directly(partial_value, "chan", 1)


def solution(mesh):
    in_specs = (
        P(("parts", "tm"), "space", None),
        P(("parts", "tm"), "space", None),
        P(),
        P(),
        P(),
        P(),
        P(),
    )
    out_specs = P(("parts", "tm"), "space", None)
    return jax.shard_map(
        per_device, mesh=mesh, in_specs=in_specs, out_specs=out_specs, check_vma=False
    )
```

profile of v0, /device:TPU:65, one launch (start us, length us, event | category | flops | bytes accessed | tf_op | source)
XLA Modules:
  0.0 110.9 jit_solution(11368657082339907676)
XLA Ops:
  1.4 7.1 %collective-permute-start = (bf16[2,4,3,128]{3,2,1,0:T(4,128)(2,1)S(1)}, bf16[2,4,3,128]{3,2,1,0:T(4,128)(2,1)S(1)}, u32[]{:S(2)}, u32[]{:S(2)}) collective-permute-start(bf16[2,4,3,128]{3,2,1,0:T(4,128)(2,1)S(1)} %get-tuple-element.20), channel_id=1, source_target_pairs={{0,1},{1,16},{16,17},{17,32},{32,33},{33,48},{48,49},{49,64},{64,6... | collective-permute-start | bytes 18440 | tf_op jit(solution)/shard_map/ppermute | solution.py:15
  8.5 37.6 %collective-permute-start.1 = (bf16[2,4,3,128]{3,2,1,0:T(4,128)(2,1)S(1)}, bf16[2,4,3,128]{3,2,1,0:T(4,128)(2,1)S(1)}, u32[]{:S(2)}, u32[]{:S(2)}) collective-permute-start(bf16[2,4,3,128]{3,2,1,0:T(4,128)(2,1)S(1)} %get-tuple-element.21), channel_id=1, source_target_pairs={{1,0},{16,1},{17,16},{32,17},{33,32},{48,33},{49,48},{64,49},{65,6... | collective-permute-start | bytes 18440 | tf_op jit(solution)/shard_map/ppermute | solution.py:16
  46.3 1.2 %fusion.113 = (bf16[1,64,1728]{2,1,0:T(8,128)(2,1)S(1)}, bf16[1,64,1728]{2,1,0:T(8,128)(2,1)S(1)}, bf16[1,64,1728]{2,1,0:T(8,128)(2,1)S(1)}) fusion(bf16[3,64,1728]{2,1,0:T(8,128)(2,1)} %param.11), kind=kLoop, calls=%fused_computation.145 | loop fusion | bytes 1327104 | tf_op jit(solution)/shard_map/slice | solution.py:104
  48.1 1.3 %copy.92 = bf16[64,64,3,3,3]{1,0,4,3,2:T(8,128)(2,1)} copy(bf16[64,64,3,3,3]{0,4,3,2,1:T(4,128)(2,1)S(1)} %squeeze.32) | data formatting | bytes 442368 | tf_op jit(solution)/shard_map/squeeze | solution.py:104
  49.9 1.4 %copy.97 = bf16[64,64,3,3,3]{1,0,4,3,2:T(8,128)(2,1)} copy(bf16[64,64,3,3,3]{0,4,3,2,1:T(4,128)(2,1)S(1)} %squeeze.34) | data formatting | bytes 442368 | tf_op jit(solution)/shard_map/squeeze | solution.py:104
  51.8 0.9 copy.102
  53.4 1.8 %copy.129 = bf16[64,4,10,1,128]{0,1,4,2,3:T(4,128)(2,1)S(1)} copy(bf16[64,4,10,1,128]{4,0,2,1,3:T(8,128)(2,1)S(1)} %maximum_bitcast_fusion.4) | data formatting | bytes 1310720
  56.9 4.3 %fusion.25 = f32[2,8,8,17,64]{4,2,3,1,0:T(8,128)S(1)} fusion(bf16[64,64,3,3,3]{1,0,4,3,2:T(8,128)(2,1)S(1)} %copy-done.3, bf16[64,4,10,1,7,2]{0,4,5,2,1,3:T(8,128)(2,1)S(1)} %slice.118, bf16[64,4,10,1,8,17]{0,4,5,2,1,3:T(8,128)(2,1)S(1)} %copy.90, pred[8,17]{0,1:T(8,128)(4,1)S(1)} %copy-done.9), kind=kOutput, calls=%fused_computation.25 | convolution fusion | flops 483770368 | bytes 1546376 | tf_op jit(solution)/shard_map/conv_general_dilated | solution.py:50
  62.4 0.8 copy-done.1
  63.2 3.2 %convolution_select_fusion.1 = f32[2,6,8,17,64]{4,2,3,1,0:T(8,128)S(1)} fusion(bf16[64,64,3,3,3]{1,0,4,3,2:T(8,128)(2,1)S(1)} %copy-done.1, bf16[64,4,8,1,7,2]{0,4,5,2,1,3:T(8,128)(2,1)S(1)} %slice.120, bf16[64,4,8,1,8,17]{0,4,5,2,1,3:T(8,128)(2,1)S(1)} %copy.95, pred[8,17]{0,1:T(8,128)(4,1)S(1)} %copy-done.9), kind=kOutput, calls=%fused_computation.28 | convolution fusion | flops 362944512 | bytes 1253512 | tf_op jit(solution)/shard_map/conv_general_dilated | solution.py:50
  67.6 1.6 %maximum_bitcast_fusion.2 = bf16[64,4,6,1,128]{0,1,4,2,3:T(4,128)(2,1)S(1)} fusion(bf16[64,1,6,128]{0,1,3,2:T(2,128)(2,1)S(1)} %broadcast.115, bf16[64,2,6,128]{0,1,3,2:T(2,128)(2,1)S(1)} %broadcast_select_fusion.1), kind=kLoop, calls=%fused_computation.69 | loop fusion | flops 1179648 | bytes 688128 | tf_op jit(solution)/shard_map/broadcast_in_dim | solution.py:51
  70.0 2.1 %convolution_select_fusion.3 = f32[2,4,8,17,64]{4,2,3,1,0:T(8,128)S(1)} fusion(bf16[64,64,3,3,3]{1,0,4,3,2:T(8,128)(2,1)S(1)} %copy.102, bf16[64,4,6,1,7,2]{0,4,5,2,1,3:T(8,128)(2,1)S(1)} %slice.122, bf16[64,4,6,1,8,17]{0,4,5,2,1,3:T(8,128)(2,1)S(1)} %copy.100, pred[8,17]{0,1:T(8,128)(4,1)S(1)} %copy-done.9), kind=kOutput, calls=%fused_computation.40 | convolution fusion | flops 242118656 | bytes 960648 | tf_op jit(solution)/shard_map/conv_general_dilated | solution.py:50
  72.6 1.3 %collective-permute-start.2 = (bf16[64,1,4,128]{3,0,2,1:T(8,128)(2,1)S(1)}, bf16[64,1,4,128]{3,0,2,1:T(8,128)(2,1)S(1)}, u32[]{:S(2)}, u32[]{:S(2)}) collective-permute-start(bf16[64,1,4,128]{3,0,2,1:T(8,128)(2,1)S(1)} %get-tuple-element.19), channel_id=1, source_target_pairs={{2,0},{4,2},{6,4},{8,6},{10,8},{12,10},{14,12},{3,1},{5,3},{7,5},{... | collective-permute-start | bytes 196616 | tf_op jit(solution)/shard_map/ppermute | solution.py:30
  73.9 4.4 %collective-permute-done.2 = bf16[64,1,4,128]{3,0,2,1:T(8,128)(2,1)S(1)} collective-permute-done((bf16[64,1,4,128]{3,0,2,1:T(8,128)(2,1)S(1)}, bf16[64,1,4,128]{3,0,2,1:T(8,128)(2,1)S(1)}, u32[]{:S(2)}, u32[]{:S(2)}) %collective-permute-start.2) | collective-permute-done | bytes 65568 | tf_op jit(solution)/shard_map/ppermute | solution.py:30
  78.3 2.0 %collective-permute-start.3 = (bf16[64,2,3,128]{3,0,2,1:T(8,128)(2,1)S(1)}, bf16[64,2,3,128]{3,0,2,1:T(8,128)(2,1)S(1)}, u32[]{:S(2)}, u32[]{:S(2)}) collective-permute-start(bf16[64,2,3,128]{3,0,2,1:T(8,128)(2,1)S(1)} %get-tuple-element.16), channel_id=1, source_target_pairs={{0,1},{1,16},{16,17},{17,32},{32,33},{33,48},{48,49},{49,64},{64,6... | collective-permute-start | bytes 294920 | tf_op jit(solution)/shard_map/ppermute | solution.py:15
  80.3 2.4 %collective-permute-start.4 = (bf16[64,2,3,128]{3,0,2,1:T(8,128)(2,1)S(1)}, bf16[64,2,3,128]{3,0,2,1:T(8,128)(2,1)S(1)}, u32[]{:S(2)}, u32[]{:S(2)}) collective-permute-start(bf16[64,2,3,128]{3,0,2,1:T(8,128)(2,1)S(1)} %get-tuple-element.17), channel_id=1, source_target_pairs={{1,0},{16,1},{17,16},{32,17},{33,32},{48,33},{49,48},{64,49},{65,6... | collective-permute-start | bytes 294920 | tf_op jit(solution)/shard_map/ppermute | solution.py:16
  82.8 3.5 %collective-permute-done.4 = bf16[64,2,3,128]{3,0,2,1:T(8,128)(2,1)S(1)} collective-permute-done((bf16[64,2,3,128]{3,0,2,1:T(8,128)(2,1)S(1)}, bf16[64,2,3,128]{3,0,2,1:T(8,128)(2,1)S(1)}, u32[]{:S(2)}, u32[]{:S(2)}) %collective-permute-start.4) | collective-permute-done | bytes 98336 | tf_op jit(solution)/shard_map/ppermute | solution.py:16
  86.5 1.6 %copy.130 = bf16[64,4,10,1,128]{0,1,4,2,3:T(4,128)(2,1)S(1)} copy(bf16[64,4,10,1,128]{4,0,2,1,3:T(8,128)(2,1)S(1)} %maximum_bitcast_fusion.5) | data formatting | bytes 1310720
  89.8 4.3 %fusion.22 = f32[2,8,8,17,64]{4,2,3,1,0:T(8,128)S(1)} fusion(bf16[64,64,3,3,3]{1,0,4,3,2:T(8,128)(2,1)S(1)} %copy-done.4, bf16[64,4,10,1,7,2]{0,4,5,2,1,3:T(8,128)(2,1)S(1)} %slice.133, bf16[64,4,10,1,8,17]{0,4,5,2,1,3:T(8,128)(2,1)S(1)} %copy.107, pred[8,17]{0,1:T(8,128)(4,1)S(1)} %copy-done.9), kind=kOutput, calls=%fused_computation.24 | convolution fusion | flops 483770368 | bytes 1546376 | tf_op jit(solution)/shard_map/conv_general_dilated | solution.py:50
  95.6 0.8 copy-done.2
  96.4 3.2 %convolution_select_fusion = f32[2,6,8,17,64]{4,2,3,1,0:T(8,128)S(1)} fusion(bf16[64,64,3,3,3]{1,0,4,3,2:T(8,128)(2,1)S(1)} %copy-done.2, bf16[64,4,8,1,7,2]{0,4,5,2,1,3:T(8,128)(2,1)S(1)} %slice.136, bf16[64,4,8,1,8,17]{0,4,5,2,1,3:T(8,128)(2,1)S(1)} %copy.113, pred[8,17]{0,1:T(8,128)(4,1)S(1)} %copy-done.9), kind=kOutput, calls=%fused_computation.27 | convolution fusion | flops 362944512 | bytes 1253512 | tf_op jit(solution)/shard_map/conv_general_dilated | solution.py:50
  101.6 1.6 %maximum_bitcast_fusion.3 = bf16[64,4,6,1,128]{0,1,4,2,3:T(4,128)(2,1)S(1)} fusion(bf16[64,1,6,128]{0,1,3,2:T(2,128)(2,1)S(1)} %copy.117, bf16[64,2,6,128]{0,1,3,2:T(2,128)(2,1)S(1)} %broadcast_select_fusion, bf16[64,1,6,128]{0,1,3,2:T(2,128)(2,1)S(1)} %copy.116), kind=kLoop, calls=%fused_computation.70 | loop fusion | flops 1179648 | bytes 786432 | tf_op jit(solution)/shard_map/broadcast_in_dim | solution.py:51
  103.8 2.1 %convolution_select_fusion.2 = f32[2,4,8,17,64]{4,2,3,1,0:T(8,128)S(1)} fusion(bf16[64,64,3,3,3]{1,0,4,3,2:T(8,128)(2,1)S(1)} %copy.102, bf16[64,4,6,1,7,2]{0,4,5,2,1,3:T(8,128)(2,1)S(1)} %slice.139, bf16[64,4,6,1,8,17]{0,4,5,2,1,3:T(8,128)(2,1)S(1)} %copy.119, pred[8,17]{0,1:T(8,128)(4,1)S(1)} %copy-done.9), kind=kOutput, calls=%fused_computation.39 | convolution fusion | flops 242118656 | bytes 960648 | tf_op jit(solution)/shard_map/conv_general_dilated | solution.py:50
  106.9 3.4 %all_to_all.5 = f32[2,4,4,128]{3,2,1,0:T(4,128)S(1)} all-to-all(f32[2,4,4,128]{3,2,1,0:T(4,128)S(1)} %broadcast_in_dim.93), channel_id=1, replica_groups=mesh['parts'=2,'space'=16,'tm'=8,'chan'=2] {'chan'}, dimensions={0} | all-to-all | bytes 32768 | tf_op jit(solution)/shard_map/all_to_all | solution.py:35
  (95 shorter events, 16.2 us)
Async XLA Ops:
  0.0 0.7 copy-start
  0.0 47.5 %copy-start.5 = (f32[3,64]{1,0:T(4,128)S(1)}, f32[3,64]{1,0:T(4,128)}, u32[]{:S(2)}) copy-start(f32[3,64]{1,0:T(4,128)} %param.12) | copy-start | bytes 2308
  1.4 51.3 %collective-permute-start = (bf16[2,4,3,128]{3,2,1,0:T(4,128)(2,1)S(1)}, bf16[2,4,3,128]{3,2,1,0:T(4,128)(2,1)S(1)}, u32[]{:S(2)}, u32[]{:S(2)}) collective-permute-start(bf16[2,4,3,128]{3,2,1,0:T(4,128)(2,1)S(1)} %get-tuple-element.20), channel_id=1, source_target_pairs={{0,1},{1,16},{16,17},{17,32},{32,33},{33,48},{48,49},{49,64},{64,6... | collective-permute-start | bytes 18440 | tf_op jit(solution)/shard_map/ppermute | solution.py:15
  8.5 44.3 %collective-permute-start.1 = (bf16[2,4,3,128]{3,2,1,0:T(4,128)(2,1)S(1)}, bf16[2,4,3,128]{3,2,1,0:T(4,128)(2,1)S(1)}, u32[]{:S(2)}, u32[]{:S(2)}) collective-permute-start(bf16[2,4,3,128]{3,2,1,0:T(4,128)(2,1)S(1)} %get-tuple-element.21), channel_id=1, source_target_pairs={{1,0},{16,1},{17,16},{32,17},{33,32},{48,33},{49,48},{64,49},{65,6... | collective-permute-start | bytes 18440 | tf_op jit(solution)/shard_map/ppermute | solution.py:16
  51.3 1.6 %copy-start.6 = (f32[4,64]{1,0:T(4,128)S(1)}, f32[4,64]{1,0:T(4,128)}, u32[]{:S(2)}) copy-start(f32[4,64]{1,0:T(4,128)} %param.9) | copy-start | bytes 3076
  51.3 1.6 %copy-start.7 = (f32[64]{0:T(128)S(1)}, f32[64]{0:T(128)}, u32[]{:S(2)}) copy-start(f32[64]{0:T(128)} %param.10) | copy-start | bytes 772
  55.9 1.0 copy-start.3
  55.9 1.0 copy-start.9
  62.2 1.0 copy-start.1
  72.6 5.7 %collective-permute-start.2 = (bf16[64,1,4,128]{3,0,2,1:T(8,128)(2,1)S(1)}, bf16[64,1,4,128]{3,0,2,1:T(8,128)(2,1)S(1)}, u32[]{:S(2)}, u32[]{:S(2)}) collective-permute-start(bf16[64,1,4,128]{3,0,2,1:T(8,128)(2,1)S(1)} %get-tuple-element.19), channel_id=1, source_target_pairs={{2,0},{4,2},{6,4},{8,6},{10,8},{12,10},{14,12},{3,1},{5,3},{7,5},{... | collective-permute-start | bytes 196616 | tf_op jit(solution)/shard_map/ppermute | solution.py:30
  78.3 4.4 %collective-permute-start.3 = (bf16[64,2,3,128]{3,0,2,1:T(8,128)(2,1)S(1)}, bf16[64,2,3,128]{3,0,2,1:T(8,128)(2,1)S(1)}, u32[]{:S(2)}, u32[]{:S(2)}) collective-permute-start(bf16[64,2,3,128]{3,0,2,1:T(8,128)(2,1)S(1)} %get-tuple-element.16), channel_id=1, source_target_pairs={{0,1},{1,16},{16,17},{17,32},{32,33},{33,48},{48,49},{49,64},{64,6... | collective-permute-start | bytes 294920 | tf_op jit(solution)/shard_map/ppermute | solution.py:15
  80.3 6.0 %collective-permute-start.4 = (bf16[64,2,3,128]{3,0,2,1:T(8,128)(2,1)S(1)}, bf16[64,2,3,128]{3,0,2,1:T(8,128)(2,1)S(1)}, u32[]{:S(2)}, u32[]{:S(2)}) collective-permute-start(bf16[64,2,3,128]{3,0,2,1:T(8,128)(2,1)S(1)} %get-tuple-element.17), channel_id=1, source_target_pairs={{1,0},{16,1},{17,16},{32,17},{33,32},{48,33},{49,48},{64,49},{65,6... | collective-permute-start | bytes 294920 | tf_op jit(solution)/shard_map/ppermute | solution.py:16
  88.8 1.0 copy-start.4
  95.4 1.0 copy-start.2
  106.1 0.7 copy-start.8
where the time goes:
time: 111 us
  starting transfers between devices  50.4 us (45%)
  local copies, waits for them, and re-layouts  22.3 us (20%)
  matrix products  19.8 us (18%)
  waiting for transfers between devices  7.89 us (7%)
  other arithmetic  6.36 us (6%)
  blocking collectives  3.41 us (3%)
    ppermute x2, starting transfers between devices, with_halo(): lax.ppermute(first, axis, [(b, a) for a, b in up])  40.1 us
    conv_general_dilated x6, matrix products, correlate(): lax.conv_general_dilated(inputs[None], kernel, (1, 1, 1), ((0, 0), (0, 0)...  19.3 us
    ppermute x2, starting transfers between devices, with_halo(): lax.ppermute(last, axis, up)  9.01 us
    unnamed x24, local copies, waits for them, and re-layouts  7.87 us
    squeeze x6, local copies, waits for them, and re-layouts, apply_layer(): summed = correlate(padded, kernels[layer])  4.42 us
    ppermute x1, waiting for transfers between devices, from_behind(): return lax.ppermute(value, axis, pairs)  4.37 us
    broadcast_in_dim x6, other arithmetic, correlate(): inputs[None]  3.9 us
    ppermute x2, waiting for transfers between devices, with_halo(): lax.ppermute(first, axis, [(b, a) for a, b in up])  3.51 us
  transfers between devices with their start and end apart: 5, of which 2 were waited for; matrix products, arithmetic and copies ran while one was open for 6% of the time, Pallas kernels for 0%

commit v1 on v0

v1 whole, which is shorter than its diff:
```python
import functools

import jax
import jax.numpy as jnp
from jax import lax
from jax.experimental import pallas as pl
from jax.experimental.pallas import tpu as pltpu
from jax.sharding import PartitionSpec as P

F32 = jnp.float32
BF16 = jnp.bfloat16
MESH = pl.DeviceIdType.MESH


def iota(shape, dim):
    return lax.broadcasted_iota(jnp.int32, shape, dim)


def three_terms(value):
    high = value.astype(BF16)
    rest = value - high.astype(F32)
    middle = rest.astype(BF16)
    low = (rest - middle.astype(F32)).astype(BF16)
    return high, middle, low


def one_hot(condition):
    return jnp.where(condition, 1.0, 0.0).astype(BF16)


def dot(a, b):
    return lax.dot_general(a, b, (((1,), (0,)), ((), ())), preferred_element_type=F32)


def dot_nt(a, b):
    return lax.dot_general(a, b, (((1,), (1,)), ((), ())), preferred_element_type=F32)


def dot_tn(a, b):
    return lax.dot_general(a, b, (((0,), (0,)), ((), ())), preferred_element_type=F32)


def quad(row):
    return jnp.concatenate([row] * 4, axis=1)


def put(ref, lead, value, count):
    width = value.shape[2]
    q = iota((count, 16, width), 1)
    last, first = value[:, 112:128], value[:, 0:16]
    before = jnp.where(q == 0, 0.0, pltpu.roll(last, 1, 1))
    after = jnp.where(q == 15, 0.0, pltpu.roll(first, 15, 1))
    ref[(*lead, pl.ds(0, count), pl.ds(0, 16))] = before.astype(BF16)
    ref[(*lead, pl.ds(0, count), pl.ds(16, 128))] = value.astype(BF16)
    ref[(*lead, pl.ds(0, count), pl.ds(144, 16))] = after.astype(BF16)


def kernel(
    spaces, times,
    ev_hbm, so_hbm, emb_hbm, gain_hbm, cw_hbm, cb_hbm, rw_hbm,
    out_ref,
    ev, so, emb, gain, cw, cb, rw,
    win, unique, ha, hb, final, paired, mine, theirs,
    load_sem, send_sem, recv_sem,
):
    space, time, core = lax.axis_index("space"), lax.axis_index("tm"), lax.axis_index("chan")
    grid_rows = 8 * spaces
    up, down = space > 0, space < spaces - 1
    later, earlier = time < times - 1, time > 0

    loads = [
        pltpu.make_async_copy(src, dst, load_sem.at[i])
        for i, (src, dst) in enumerate(
            ((ev_hbm, ev), (so_hbm, so), (cw_hbm, cw), (emb_hbm, emb), (gain_hbm, gain), (cb_hbm, cb), (rw_hbm, rw))
        )
    ]
    for load in loads:
        load.start()

    barrier = pltpu.get_barrier_semaphore()

    def greet(there, device):
        @pl.when(there)
        def _():
            pl.semaphore_signal(barrier, inc=1, device_id=device, device_id_type=MESH)

    greet(up, {"space": space - 1})
    greet(down, {"space": space + 1})
    greet(later, {"tm": time + 1})
    greet(earlier, {"tm": time - 1})
    pl.semaphore_signal(barrier, inc=1, device_id={"chan": 1 - core}, device_id_type=MESH)

    spread = one_hot(iota((128, 128), 0) == (iota((128, 128), 1) & 15) * 8 + (iota((128, 128), 1) >> 4))
    m = iota((64, 64), 0)
    source = (
        (m & 1) * 32 + ((m >> 5) * 2 + 1 - ((m >> 2) & 1)) * 8 + ((m >> 3) & 3) * 2 + ((m >> 1) & 1)
    )
    order = one_hot(iota((64, 64), 1) == source)
    loads[0].wait()
    loads[1].wait()
    raw = jnp.concatenate([ev[...].astype(F32).reshape(32, 128), so[...].astype(F32).reshape(32, 128)], axis=0)
    staged = dot(order, dot(raw.astype(BF16), spread).astype(BF16)).reshape(2, 4, 8, 128).astype(BF16)
    win[0, 3:7] = staged[0]
    win[1, 3:7] = staged[1]

    def remote(src, dst, i, device):
        return pltpu.make_async_remote_copy(
            src_ref=src, dst_ref=dst, send_sem=send_sem.at[i], recv_sem=recv_sem.at[i],
            device_id=device, device_id_type=MESH,
        )

    to_below = remote(win.at[0:2, 4:7], win.at[0:2, 0:3], 0, {"space": space + 1})
    to_above = remote(win.at[0:2, 3:6], win.at[0:2, 7:10], 1, {"space": space - 1})
    to_earlier = remote(win.at[0, 3:7], win.at[2, 3:7], 2, {"tm": time - 1})
    on_below = remote(win.at[2, 4:7], win.at[2, 0:3], 3, {"space": space + 1})
    on_above = remote(win.at[2, 3:6], win.at[2, 7:10], 4, {"space": space - 1})
    swap = remote(mine, theirs, 5, {"chan": 1 - core})

    pl.semaphore_wait(
        barrier,
        1 + jnp.where(up, 1, 0) + jnp.where(down, 1, 0) + jnp.where(later, 1, 0) + jnp.where(earlier, 1, 0),
    )
    pl.when(down)(to_below.start)
    pl.when(up)(to_above.start)
    pl.when(earlier)(to_earlier.start)

    loads[2].wait()
    blank = jnp.zeros((3, 1, 3, 16, 128), F32)
    for half in range(4):
        pieces = []
        for chunk in (2 * half, 2 * half + 1):
            begin = 216 * chunk // 128 * 128
            stop = min(-(-(216 * chunk + 216) // 128) * 128, cw.shape[2])
            n = iota((216, stop - begin), 0)
            select = one_hot(iota((216, stop - begin), 1) == (n & 7) * 27 + (n >> 3) + (216 * chunk - begin))
            taps = [cw[layer, :, begin:stop] for layer in range(3)]
            two = dot_nt(select, jnp.concatenate([taps[0], taps[0], taps[1], taps[1]], axis=0))
            one = dot_nt(select, jnp.concatenate([taps[2], taps[2]], axis=0))
            pieces.append([v.reshape(27, 8, 128) for v in (two[:, :128], two[:, 128:], one)])
        for layer in range(3):
            tap = jnp.concatenate([pieces[0][layer], pieces[1][layer]], axis=1).reshape(3, 3, 3, 16, 128)
            low = jnp.concatenate([tap, blank], axis=1)
            high = jnp.concatenate([blank, tap], axis=1)
            both = jnp.where(iota((3, 4, 3, 16, 128), 4) < 64, low, high)
            unique[layer, :, :, :, 16 * half : 16 * half + 16, :] = both.astype(BF16)

    for load in loads[3:]:
        load.wait()
    e_terms = three_terms(quad(emb[...]))
    g_terms = three_terms(quad(gain[...]))
    column = jnp.concatenate(
        [t.astype(F32) for t in e_terms] + [t.astype(F32) for t in g_terms] + [jnp.zeros((1, 256), F32)], axis=0
    )
    make = jnp.where(
        iota((64, 256), 0) >> 4 == iota((64, 256), 1) >> 6, jnp.concatenate([column] * 4, axis=0), 0.0
    ).astype(BF16)
    bias = [quad(cb[layer : layer + 1, :]) for layer in range(3)]

    base = 8 * space + 4 * core
    k = iota((16, 128), 0)
    column_parity = iota((16, 128), 1) >> 4

    def inputs(cell, row, there):
        event, signal = cell
        inside = (row >= 0) & (row < grid_rows) & there
        code = 2 * ((column_parity + row) & 1) + event.astype(jnp.int32)
        value = jnp.where(k < 12, jnp.where(code == (k & 3), 1.0, 0.0), jnp.where(k < 15, signal, 0.0))
        return jnp.where(inside, value, 0.0)

    def start(cells, count, first_row, there):
        columns = []
        for j in range(count):
            blocks = []
            for b in range(4):
                blocks.append(inputs(cells(j, b), first_row + 2 * j + (b & 1), there))
            columns.append(jnp.concatenate(blocks, axis=0).astype(BF16))
        return dot_tn(jnp.concatenate(columns, axis=1), make).reshape(count, 128, 256)

    def taps_of(ref, lead, first, count):
        parts = []
        for shift in range(3):
            for pair in range(2):
                part = ref[(*lead, pl.ds(first + pair, count), pl.ds(16 * shift, 128))]
                parts.append(part.reshape(count * 128, part.shape[-1]))
        return parts

    def within(layer):
        rows = []
        for shift in range(3):
            for pair in range(2):
                for r in (1, 0):
                    for y in range(2):
                        rows.append(
                            jnp.concatenate(
                                [unique[layer, r + 1 - to, 2 * pair + y, shift] for to in (1, 0)], axis=1
                            )
                        )
        return jnp.concatenate(rows, axis=0)

    def across(layer):
        rows = []
        none = jnp.zeros((64, 128), BF16)
        for shift in range(3):
            for pair in range(2):
                for y in range(2):
                    rows.append(jnp.concatenate([none, unique[layer, 0, 2 * pair + y, shift]], axis=1))
                for y in range(2):
                    rows.append(jnp.concatenate([unique[layer, 2, 2 * pair + y, shift], none], axis=1))
        return jnp.concatenate(rows, axis=0)

    def finish(total, layer, count, first_row, there):
        row = first_row + 2 * iota((count, 1, 256), 0) + ((iota((count, 1, 256), 2) >> 6) & 1)
        inside = (row >= 0) & (row < grid_rows) & there
        value = jnp.maximum(total + bias[layer], 0.0).reshape(count, 128, 256)
        return value * jnp.where(inside, 1.0, 0.0)

    pl.when(later)(to_earlier.wait_recv)
    pl.when(later & down)(on_below.start)
    pl.when(later & up)(on_above.start)
    pl.when(up)(to_below.wait_recv)
    pl.when(down)(to_above.wait_recv)

    def first_kind(w, carry):
        there = (w == 0) | later

        @pl.when((w == 1) & later & up)
        def _():
            on_below.wait_recv()

        @pl.when((w == 1) & later & down)
        def _():
            on_above.wait_recv()

        def cells(j, b):
            tile = win[2 * w, 2 * core + j].astype(F32)
            return tile[2 * b : 2 * b + 1], tile[2 * b + 1 : 2 * b + 2]

        put(ha, (), start(cells, 8, base - 6, there), 8)
        total = dot(jnp.concatenate(taps_of(ha, (), 0, 7), axis=1), within(0))
        put(hb, (), finish(total, 0, 7, base - 5, there), 7)
        total = dot(jnp.concatenate(taps_of(hb, (), 0, 6), axis=1), within(1))
        put(ha, (), finish(total, 1, 6, base - 4, there), 6)
        total = dot(jnp.concatenate(taps_of(ha, (), 0, 5), axis=1), within(2))
        value = finish(total, 2, 5, base - 3, there)
        put(final, (w,), value, 5)
        swapped = jnp.where((iota((4, 128, 256), 2) & 64) == 0, value[1:5], value[0:4])
        put(
            paired, (w,),
            jnp.concatenate([pltpu.roll(swapped[:, :, :128], 64, 2), pltpu.roll(swapped[:, :, 128:], 64, 2)], axis=2),
            4,
        )
        return carry

    lax.fori_loop(0, 2, first_kind, 0)

    def beside(ref, first, count):
        left = taps_of(ref.at[0, :, :, 0:128], (), first, count)
        right = taps_of(ref.at[1, :, :, 128:256], (), first, count)
        return [v for pair in zip(left, right) for v in pair]

    def second(own, others, layer, count, first_other):
        lhs = jnp.concatenate(taps_of(own, (), 0, count) + beside(others, first_other, count), axis=1)
        return dot(lhs, jnp.concatenate([within(layer), across(layer)], axis=0))

    def late_cells(j, b):
        tile = win[1, 2 * core + 1 + j + (b & 1)].astype(F32)
        at = (b >> 1) * 4 + (1 - (b & 1)) * 2
        return tile[at : at + 1], tile[at + 1 : at + 2]

    put(ha, (), start(late_cells, 5, base - 3, True), 5)
    put(hb, (), finish(second(ha, final, 0, 4, 0), 0, 4, base - 2, True), 4)
    put(ha, (), finish(second(hb, paired, 1, 3, 0), 1, 3, base - 1, True), 3)
    last = finish(second(ha, final, 2, 2, 1), 2, 2, base, True).astype(BF16).reshape(256, 256)

    w_terms = three_terms(quad(rw[...]))
    n = iota((32, 256), 0)
    weight = jnp.where(n >> 3 == 0, w_terms[0].astype(F32), jnp.where(n >> 3 == 1, w_terms[1].astype(F32), w_terms[2].astype(F32)))
    weight = jnp.where((n < 24) & ((n & 7) == iota((32, 256), 1) >> 6), weight, 0.0).astype(BF16)
    a_sum = dot_nt(weight, final[0, 1:4, 16:144, :].reshape(384, 256))
    b_sum = dot_nt(weight, last)
    a_sum = a_sum[0:8] + a_sum[8:16] + a_sum[16:24]
    b_sum = b_sum[0:8] + b_sum[8:16] + b_sum[16:24]
    y = iota((8, 128), 0) & 3
    rounds = []
    for total, shift in ((a_sum, 1), (b_sum, 0)):
        for r in range(2):
            rows = []
            for i in range(4):
                pair, inner = (i + shift) // 2, (i + shift) % 2
                b = (1 - r) * 2 + inner
                rows.append(jnp.broadcast_to(total[b : b + 1, 128 * pair : 128 * pair + 128], (8, 128)))
            rounds.append(jnp.where(y < 2, jnp.where(y == 0, rows[0], rows[1]), jnp.where(y == 2, rows[2], rows[3])))
    logits = jnp.concatenate(rounds, axis=0)
    back = one_hot(iota((128, 128), 1) == (iota((128, 128), 0) & 15) * 8 + (iota((128, 128), 0) >> 4))
    parts = dot(jnp.concatenate(three_terms(logits), axis=0), back)
    logits = (parts[0:32] + parts[32:64] + parts[64:96]).reshape(4, 8, 128)
    mine[...] = logits
    swap.start()
    swap.wait_recv()
    own = (iota((4, 8, 128), 1) >> 2) == core
    out_ref[...] = jnp.where(own, logits, theirs[...])

    pl.when(down)(to_below.wait_send)
    pl.when(up)(to_above.wait_send)
    pl.when(earlier)(to_earlier.wait_send)
    pl.when(later & down)(on_below.wait_send)
    pl.when(later & up)(on_above.wait_send)
    swap.wait_send()


def per_device(spaces, times, events, soft_info, embed, soft_gain, conv_weights, conv_bias, readout_weight):
    layers, channels, taps = conv_weights.shape
    gain = soft_gain.reshape(1, channels)
    readout = readout_weight.reshape(1, channels)
    any_space = pl.BlockSpec(memory_space=pl.ANY)
    return pl.pallas_call(
        functools.partial(kernel, spaces, times),
        out_shape=jax.ShapeDtypeStruct(events.shape, F32),
        in_specs=[any_space] * 7,
        out_specs=pl.BlockSpec(memory_space=pltpu.VMEM),
        scratch_shapes=[
            pltpu.VMEM(events.shape, jnp.int32),
            pltpu.VMEM(soft_info.shape, BF16),
            pltpu.VMEM(embed.shape, F32),
            pltpu.VMEM(gain.shape, F32),
            pltpu.VMEM(conv_weights.shape, BF16),
            pltpu.VMEM(conv_bias.shape, F32),
            pltpu.VMEM(readout.shape, F32),
            pltpu.VMEM((3, 10, 8, 128), BF16),
            pltpu.VMEM((layers, 3, 4, 3, channels, 128), BF16),
            pltpu.VMEM((8, 160, 256), BF16),
            pltpu.VMEM((7, 160, 256), BF16),
            pltpu.VMEM((2, 5, 160, 256), BF16),
            pltpu.VMEM((2, 4, 160, 256), BF16),
            pltpu.VMEM(events.shape, F32),
            pltpu.VMEM(events.shape, F32),
            pltpu.SemaphoreType.DMA((7,)),
            pltpu.SemaphoreType.DMA((6,)),
            pltpu.SemaphoreType.DMA((6,)),
        ],
        compiler_params=pltpu.CompilerParams(collective_id=0, has_side_effects=True, vmem_limit_bytes=48 * 1024 * 1024),
    )(events, soft_info, embed, gain, conv_weights, conv_bias, readout)


def solution(mesh):
    tiled = P(("parts", "tm"), "space", None)
    return jax.shard_map(
        functools.partial(per_device, mesh.shape["space"], mesh.shape["tm"]),
        mesh=mesh, in_specs=(tiled, tiled, P(), P(), P(), P(), P()), out_specs=tiled, check_vma=False,
    )
```

time: 111 us -> 62.9 us (0.57)
  Pallas kernels: 0 us -> 58.1 us
  starting transfers between devices: 50.4 us -> 0 us
  matrix products: 19.8 us -> 0 us
  local copies, waits for them, and re-layouts: 22.3 us -> 4.48 us
  waiting for transfers between devices: 7.89 us -> 0 us
  other arithmetic: 6.36 us -> 0 us
  blocking collectives: 3.41 us -> 0 us
    pallas_call x0 -> x1, Pallas kernels: none -> 58.1 us  [per_device(): pl.pallas_call(functools.partial(kernel, spaces, times), out_shape=jax.Sh...]
    ppermute x5 -> x0, starting transfers between devices: 50.4 us -> none  [the longest x2 40.1 us: with_halo(): lax.ppermute(first, axis, [(b, a) for a, b in up])]
    conv_general_dilated x6 -> x0, matrix products: 19.3 us -> none  [correlate(): lax.conv_general_dilated(inputs[None], kernel, (1, 1, 1), ((0, 0), (0, 0)...]
    ppermute x5 -> x0, waiting for transfers between devices: 7.89 us -> none  [the longest x1 4.37 us: from_behind(): return lax.ppermute(value, axis, pairs)]
    squeeze x6 -> x0, local copies, waits for them, and re-layouts: 4.42 us -> none  [apply_layer(): summed = correlate(padded, kernels[layer])]
    broadcast_in_dim x6 -> x0, other arithmetic: 3.9 us -> none  [correlate(): inputs[None]]
    slice x13 -> x0, local copies, waits for them, and re-layouts: 3.54 us -> none  [the longest x4 2.01 us: apply_layer(): summed = correlate(padded, kernels[layer])]
    all_to_all x1 -> x0, blocking collectives: 3.41 us -> none  [from_everyone(): return lax.all_to_all(copies, axis, split_axis=0, concat_axis=0, tiled=True)]
  transfers between devices with their start and end apart: 5 -> 0, of which waited for: 2 -> 0; matrix products, arithmetic and copies ran while one was open for 6% -> 0% of each run, Pallas kernels for 0% -> 0%
where the time goes in v1:
time: 62.9 us; the launch traced here: 62.7 us
  Pallas kernels  58.1 us (92%)
  local copies, waits for them, and re-layouts  4.48 us (7%)
    pallas_call x1, Pallas kernels, per_device(): pl.pallas_call(functools.partial(kernel, spaces, times), out_shape=jax.Sh...  58.1 us
    unnamed x15, local copies, waits for them, and re-layouts  4.48 us

profile of v1, /device:TPU:65, one launch (start us, length us, event | category | flops | bytes accessed | tf_op | source)
XLA Modules:
  0.0 62.7 jit_solution(10668127267438542148)
XLA Ops:
  0.0 0.0 copy-start.3
  0.0 0.0 copy-start.5
  0.0 0.0 copy-start.6
  0.0 0.7 %copy-done.3 = f32[4,64]{1,0:T(4,128)S(1)} copy-done((f32[4,64]{1,0:T(4,128)S(1)}, f32[4,64]{1,0:T(4,128)}, u32[]{:S(2)}) %copy-start.3) | copy-done | bytes 1048
  0.7 0.0 copy-done.5
  0.7 0.0 copy-done.6
  0.7 0.0 copy-start
  0.7 1.1 %copy-done = bf16[3,64,1728]{2,1,0:T(8,128)(2,1)S(1)} copy-done((bf16[3,64,1728]{2,1,0:T(8,128)(2,1)S(1)}, bf16[3,64,1728]{2,1,0:T(8,128)(2,1)}, u32[]{:S(2)}) %copy-start) | copy-done | bytes 663576
  1.8 0.0 copy-start.1
  1.8 0.7 %copy-done.1 = s32[4,8,128]{2,1,0:T(8,128)S(1)} copy-done((s32[4,8,128]{2,1,0:T(8,128)S(1)}, s32[4,8,128]{2,1,0:T(8,128)}, u32[]{:S(2)}) %copy-start.1) | copy-done | bytes 16408
  2.5 0.0 copy-start.2
  2.5 0.7 %copy-done.2 = bf16[4,8,128]{2,1,0:T(8,128)(2,1)S(1)} copy-done((bf16[4,8,128]{2,1,0:T(8,128)(2,1)S(1)}, bf16[4,8,128]{2,1,0:T(8,128)(2,1)}, u32[]{:S(2)}) %copy-start.2) | copy-done | bytes 8216
  3.2 0.0 copy-start.4
  3.2 0.7 %copy-done.4 = f32[3,64]{1,0:T(4,128)S(1)} copy-done((f32[3,64]{1,0:T(4,128)S(1)}, f32[3,64]{1,0:T(4,128)}, u32[]{:S(2)}) %copy-start.4) | copy-done | bytes 792
  3.9 58.1 %shard_map.73 = f32[4,8,128]{2,1,0:T(8,128)S(1)} custom-call(s32[4,8,128]{2,1,0:T(8,128)S(1)} %copy-done.1, bf16[4,8,128]{2,1,0:T(8,128)(2,1)S(1)} %copy-done.2, f32[4,64]{1,0:T(4,128)S(1)} %copy-done.3, f32[1,64]{1,0:T(1,128)S(1)} %bitcast.2, bf16[3,64,1728]{2,1,0:T(8,128)(2,1)S(1)} %copy-done, f32[3,64]{1,0:T(4,128)S(1)} %copy-done.4, f32[1,64]{1,0:T(1,128)S(1)} %bitcast.3), custom_call_target="tpu_custom_call" | custom-call | tf_op jit(solution)/shard_map/pallas_call | solution.py:316
  62.0 0.6 copy.9
Async XLA Ops:
  0.0 0.7 %copy-start.3 = (f32[4,64]{1,0:T(4,128)S(1)}, f32[4,64]{1,0:T(4,128)}, u32[]{:S(2)}) copy-start(f32[4,64]{1,0:T(4,128)} %emb_hbm.1) | copy-start | bytes 3076
  0.0 0.7 %copy-start.5 = (f32[64]{0:T(128)S(1)}, f32[64]{0:T(128)}, u32[]{:S(2)}) copy-start(f32[64]{0:T(128)} %param.10) | copy-start | bytes 772
  0.0 0.7 %copy-start.6 = (f32[64]{0:T(128)S(1)}, f32[64]{0:T(128)}, u32[]{:S(2)}) copy-start(f32[64]{0:T(128)} %param.13) | copy-start | bytes 772
  0.7 1.1 %copy-start = (bf16[3,64,1728]{2,1,0:T(8,128)(2,1)S(1)}, bf16[3,64,1728]{2,1,0:T(8,128)(2,1)}, u32[]{:S(2)}) copy-start(bf16[3,64,1728]{2,1,0:T(8,128)(2,1)} %cw_hbm.1) | copy-start | bytes 1990660
  1.8 0.7 %copy-start.1 = (s32[4,8,128]{2,1,0:T(8,128)S(1)}, s32[4,8,128]{2,1,0:T(8,128)}, u32[]{:S(2)}) copy-start(s32[4,8,128]{2,1,0:T(8,128)} %ev_hbm.1) | copy-start | bytes 49156
  2.5 0.7 %copy-start.2 = (bf16[4,8,128]{2,1,0:T(8,128)(2,1)S(1)}, bf16[4,8,128]{2,1,0:T(8,128)(2,1)}, u32[]{:S(2)}) copy-start(bf16[4,8,128]{2,1,0:T(8,128)(2,1)} %so_hbm.1) | copy-start | bytes 24580
  3.2 0.7 %copy-start.4 = (f32[3,64]{1,0:T(4,128)S(1)}, f32[3,64]{1,0:T(4,128)}, u32[]{:S(2)}) copy-start(f32[3,64]{1,0:T(4,128)} %cb_hbm.1) | copy-start | bytes 2308

commit v2 on v1

--- a/solution.py
+++ b/solution.py
@@ -10,6 +10,7 @@
 F32 = jnp.float32
 BF16 = jnp.bfloat16
 MESH = pl.DeviceIdType.MESH
+LEAD = 3
 
 
 def iota(shape, dim):
@@ -55,41 +56,10 @@
     ref[(*lead, pl.ds(0, count), pl.ds(144, 16))] = after.astype(BF16)
 
 
-def kernel(
-    spaces, times,
-    ev_hbm, so_hbm, emb_hbm, gain_hbm, cw_hbm, cb_hbm, rw_hbm,
-    out_ref,
-    ev, so, emb, gain, cw, cb, rw,
-    win, unique, ha, hb, final, paired, mine, theirs,
-    load_sem, send_sem, recv_sem,
+def compute(
+    spaces, space, time, up, down, later, earlier, barrier, grid_rows, remote, loads,
+    out_ref, ev, so, emb, gain, cw, cb, rw, win, unique, ha, hb, final, paired, result,
 ):
-    space, time, core = lax.axis_index("space"), lax.axis_index("tm"), lax.axis_index("chan")
-    grid_rows = 8 * spaces
-    up, down = space > 0, space < spaces - 1
-    later, earlier = time < times - 1, time > 0
-
-    loads = [
-        pltpu.make_async_copy(src, dst, load_sem.at[i])
-        for i, (src, dst) in enumerate(
-            ((ev_hbm, ev), (so_hbm, so), (cw_hbm, cw), (emb_hbm, emb), (gain_hbm, gain), (cb_hbm, cb), (rw_hbm, rw))
-        )
-    ]
-    for load in loads:
-        load.start()
-
-    barrier = pltpu.get_barrier_semaphore()
-
-    def greet(there, device):
-        @pl.when(there)
-        def _():
-            pl.semaphore_signal(barrier, inc=1, device_id=device, device_id_type=MESH)
-
-    greet(up, {"space": space - 1})
-    greet(down, {"space": space + 1})
-    greet(later, {"tm": time + 1})
-    greet(earlier, {"tm": time - 1})
-    pl.semaphore_signal(barrier, inc=1, device_id={"chan": 1 - core}, device_id_type=MESH)
-
     spread = one_hot(iota((128, 128), 0) == (iota((128, 128), 1) & 15) * 8 + (iota((128, 128), 1) >> 4))
     m = iota((64, 64), 0)
     source = (
@@ -103,22 +73,15 @@
     win[0, 3:7] = staged[0]
     win[1, 3:7] = staged[1]
 
-    def remote(src, dst, i, device):
-        return pltpu.make_async_remote_copy(
-            src_ref=src, dst_ref=dst, send_sem=send_sem.at[i], recv_sem=recv_sem.at[i],
-            device_id=device, device_id_type=MESH,
-        )
-
-    to_below = remote(win.at[0:2, 4:7], win.at[0:2, 0:3], 0, {"space": space + 1})
-    to_above = remote(win.at[0:2, 3:6], win.at[0:2, 7:10], 1, {"space": space - 1})
-    to_earlier = remote(win.at[0, 3:7], win.at[2, 3:7], 2, {"tm": time - 1})
-    on_below = remote(win.at[2, 4:7], win.at[2, 0:3], 3, {"space": space + 1})
-    on_above = remote(win.at[2, 3:6], win.at[2, 7:10], 4, {"space": space - 1})
-    swap = remote(mine, theirs, 5, {"chan": 1 - core})
+    to_below = remote(win.at[0:2, 4:7], win.at[0:2, 0:3], 0, 0, {"space": space + 1})
+    to_above = remote(win.at[0:2, 3:6], win.at[0:2, 7:10], 1, 1, {"space": space - 1})
+    to_earlier = remote(win.at[0, 3:7], win.at[2, 3:7], 2, 2, {"tm": time - 1})
+    on_below = remote(win.at[2, 4:7], win.at[2, 0:3], 3, 3, {"space": space + 1})
+    on_above = remote(win.at[2, 3:6], win.at[2, 7:10], 4, 4, {"space": space - 1})
 
     pl.semaphore_wait(
         barrier,
-        1 + jnp.where(up, 1, 0) + jnp.where(down, 1, 0) + jnp.where(later, 1, 0) + jnp.where(earlier, 1, 0),
+        jnp.where(up, 1, 0) + jnp.where(down, 1, 0) + jnp.where(later, 1, 0) + jnp.where(earlier, 1, 0),
     )
     pl.when(down)(to_below.start)
     pl.when(up)(to_above.start)
@@ -156,7 +119,7 @@
     ).astype(BF16)
     bias = [quad(cb[layer : layer + 1, :]) for layer in range(3)]
 
-    base = 8 * space + 4 * core
+    base = 8 * space
     k = iota((16, 128), 0)
     column_parity = iota((16, 128), 1) >> 4
 
@@ -232,22 +195,22 @@
             on_above.wait_recv()
 
         def cells(j, b):
-            tile = win[2 * w, 2 * core + j].astype(F32)
+            tile = win[2 * w, j].astype(F32)
             return tile[2 * b : 2 * b + 1], tile[2 * b + 1 : 2 * b + 2]
 
-        put(ha, (), start(cells, 8, base - 6, there), 8)
-        total = dot(jnp.concatenate(taps_of(ha, (), 0, 7), axis=1), within(0))
-        put(hb, (), finish(total, 0, 7, base - 5, there), 7)
-        total = dot(jnp.concatenate(taps_of(hb, (), 0, 6), axis=1), within(1))
-        put(ha, (), finish(total, 1, 6, base - 4, there), 6)
-        total = dot(jnp.concatenate(taps_of(ha, (), 0, 5), axis=1), within(2))
-        value = finish(total, 2, 5, base - 3, there)
-        put(final, (w,), value, 5)
-        swapped = jnp.where((iota((4, 128, 256), 2) & 64) == 0, value[1:5], value[0:4])
+        put(ha, (), start(cells, 10, base - 6, there), 10)
+        total = dot(jnp.concatenate(taps_of(ha, (), 0, 9), axis=1), within(0))
+        put(hb, (), finish(total, 0, 9, base - 5, there), 9)
+        total = dot(jnp.concatenate(taps_of(hb, (), 0, 8), axis=1), within(1))
+        put(ha, (), finish(total, 1, 8, base - 4, there), 8)
+        total = dot(jnp.concatenate(taps_of(ha, (), 0, 7), axis=1), within(2))
+        value = finish(total, 2, 7, base - 3, there)
+        put(final, (w,), value, 7)
+        swapped = jnp.where((iota((6, 128, 256), 2) & 64) == 0, value[1:7], value[0:6])
         put(
             paired, (w,),
             jnp.concatenate([pltpu.roll(swapped[:, :, :128], 64, 2), pltpu.roll(swapped[:, :, 128:], 64, 2)], axis=2),
-            4,
+            6,
         )
         return carry
 
@@ -263,58 +226,141 @@
         return dot(lhs, jnp.concatenate([within(layer), across(layer)], axis=0))
 
     def late_cells(j, b):
-        tile = win[1, 2 * core + 1 + j + (b & 1)].astype(F32)
+        tile = win[1, 1 + j + (b & 1)].astype(F32)
         at = (b >> 1) * 4 + (1 - (b & 1)) * 2
         return tile[at : at + 1], tile[at + 1 : at + 2]
 
-    put(ha, (), start(late_cells, 5, base - 3, True), 5)
-    put(hb, (), finish(second(ha, final, 0, 4, 0), 0, 4, base - 2, True), 4)
-    put(ha, (), finish(second(hb, paired, 1, 3, 0), 1, 3, base - 1, True), 3)
-    last = finish(second(ha, final, 2, 2, 1), 2, 2, base, True).astype(BF16).reshape(256, 256)
+    put(ha, (), start(late_cells, 7, base - 3, True), 7)
+    put(hb, (), finish(second(ha, final, 0, 6, 0), 0, 6, base - 2, True), 6)
+    put(ha, (), finish(second(hb, paired, 1, 5, 0), 1, 5, base - 1, True), 5)
+    last = finish(second(ha, final, 2, 4, 1), 2, 4, base, True).astype(BF16).reshape(512, 256)
 
     w_terms = three_terms(quad(rw[...]))
     n = iota((32, 256), 0)
     weight = jnp.where(n >> 3 == 0, w_terms[0].astype(F32), jnp.where(n >> 3 == 1, w_terms[1].astype(F32), w_terms[2].astype(F32)))
     weight = jnp.where((n < 24) & ((n & 7) == iota((32, 256), 1) >> 6), weight, 0.0).astype(BF16)
-    a_sum = dot_nt(weight, final[0, 1:4, 16:144, :].reshape(384, 256))
+    a_sum = dot_nt(weight, final[0, 1:6, 16:144, :].reshape(640, 256))
     b_sum = dot_nt(weight, last)
     a_sum = a_sum[0:8] + a_sum[8:16] + a_sum[16:24]
     b_sum = b_sum[0:8] + b_sum[8:16] + b_sum[16:24]
-    y = iota((8, 128), 0) & 3
+    y = iota((8, 128), 0)
     rounds = []
     for total, shift in ((a_sum, 1), (b_sum, 0)):
         for r in range(2):
-            rows = []
-            for i in range(4):
+            tile = jnp.zeros((8, 128), F32)
+            for i in range(8):
                 pair, inner = (i + shift) // 2, (i + shift) % 2
                 b = (1 - r) * 2 + inner
-                rows.append(jnp.broadcast_to(total[b : b + 1, 128 * pair : 128 * pair + 128], (8, 128)))
-            rounds.append(jnp.where(y < 2, jnp.where(y == 0, rows[0], rows[1]), jnp.where(y == 2, rows[2], rows[3])))
+                row = jnp.broadcast_to(total[b : b + 1, 128 * pair : 128 * pair + 128], (8, 128))
+                tile = jnp.where(y == i, row, tile)
+            rounds.append(tile)
     logits = jnp.concatenate(rounds, axis=0)
     back = one_hot(iota((128, 128), 1) == (iota((128, 128), 0) & 15) * 8 + (iota((128, 128), 0) >> 4))
     parts = dot(jnp.concatenate(three_terms(logits), axis=0), back)
     logits = (parts[0:32] + parts[32:64] + parts[64:96]).reshape(4, 8, 128)
-    mine[...] = logits
-    swap.start()
-    swap.wait_recv()
-    own = (iota((4, 8, 128), 1) >> 2) == core
-    out_ref[...] = jnp.where(own, logits, theirs[...])
+    result[0] = logits
+    out_ref[...] = logits
 
     pl.when(down)(to_below.wait_send)
     pl.when(up)(to_above.wait_send)
     pl.when(earlier)(to_earlier.wait_send)
     pl.when(later & down)(on_below.wait_send)
     pl.when(later & up)(on_above.wait_send)
-    swap.wait_send()
+
+
+def kernel(
+    spaces, times, lead,
+    ev_hbm, so_hbm, emb_hbm, gain_hbm, cw_hbm, cb_hbm, rw_hbm,
+    out_ref,
+    ev, so, emb, gain, cw, cb, rw,
+    win, unique, ha, hb, final, paired, result,
+    load_sem, send_sem, recv_sem, hello,
+):
+    space, time, core = lax.axis_index("space"), lax.axis_index("tm"), lax.axis_index("chan")
+    worker = core == lax.axis_size("chan") - 1
+    grid_rows = 8 * spaces
+    up, down = space > 0, space < spaces - 1
+    later, earlier = time < times - 1, time > 0
+    barrier = pltpu.get_barrier_semaphore()
+
+    def remote(src, dst, sent, got, device):
+        return pltpu.make_async_remote_copy(
+            src_ref=src, dst_ref=dst, send_sem=send_sem.at[sent], recv_sem=recv_sem.at[got],
+            device_id=device, device_id_type=MESH,
+        )
+
+    def serves(j):
+        return space >= j if j == lead else (space >= j) & (space == spaces - 1)
+
+    gives = [
+        remote(result.at[j], result.at[0], 5 + lead + j, 5, {"space": space - j, "chan": core - 1}) for j in range(lead + 1)
+    ]
+
+    @pl.when(jnp.logical_not(worker))
+    def _():
+        pl.semaphore_wait(barrier, 1)
+        for j in range(lead + 1):
+            @pl.when(space + lead <= spaces - 1 if j == lead else space == spaces - 1 - j)
+            def _():
+                pl.semaphore_signal(
+                    hello.at[j], inc=1, device_id={"space": space + j, "chan": core + 1}, device_id_type=MESH
+                )
+        gives[0].wait_recv()
+        out_ref[...] = result[0]
+
+    @pl.when(worker)
+    def _():
+        loads = [
+            pltpu.make_async_copy(src, dst, load_sem.at[i])
+            for i, (src, dst) in enumerate(
+                ((ev_hbm, ev), (so_hbm, so), (cw_hbm, cw), (emb_hbm, emb), (gain_hbm, gain), (cb_hbm, cb), (rw_hbm, rw))
+            )
+        ]
+        for load in loads:
+            load.start()
+
+        def greet(there, device):
+            @pl.when(there)
+            def _():
+                pl.semaphore_signal(barrier, inc=1, device_id=device, device_id_type=MESH)
+
+        greet(up, {"space": space - 1})
+        greet(down, {"space": space + 1})
+        greet(later, {"tm": time + 1})
+        greet(earlier, {"tm": time - 1})
+        for j in range(lead + 1):
+            greet(serves(j), {"space": space - j, "chan": core - 1})
+
+        compute(
+            spaces, space, time, up, down, later, earlier, barrier, grid_rows, remote, loads,
+            out_ref, ev, so, emb, gain, cw, cb, rw, win, unique, ha, hb, final, paired, result,
+        )
+
+        passes = [remote(result.at[j], result.at[j + 1], 5 + j, 6 + j, {"space": space + 1}) for j in range(lead)]
+        for j in range(lead + 1):
+            if j > 0:
+                pl.when(space >= j)(passes[j - 1].wait_recv)
+            if j < lead:
+                pl.when(down & (space >= j))(passes[j].start)
+        for j in range(lead + 1):
+            @pl.when(serves(j))
+            def _():
+                pl.semaphore_wait(hello.at[j], 1)
+                gives[j].start()
+        for j in range(lead):
+            pl.when(down & (space >= j))(passes[j].wait_send)
+        for j in range(lead + 1):
+            pl.when(serves(j))(gives[j].wait_send)
 
 
 def per_device(spaces, times, events, soft_info, embed, soft_gain, conv_weights, conv_bias, readout_weight):
     layers, channels, taps = conv_weights.shape
     gain = soft_gain.reshape(1, channels)
     readout = readout_weight.reshape(1, channels)
+    lead = min(LEAD, spaces - 1)
     any_space = pl.BlockSpec(memory_space=pl.ANY)
     return pl.pallas_call(
-        functools.partial(kernel, spaces, times),
+        functools.partial(kernel, spaces, times, lead),
         out_shape=jax.ShapeDtypeStruct(events.shape, F32),
         in_specs=[any_space] * 7,
         out_specs=pl.BlockSpec(memory_space=pltpu.VMEM),
@@ -328,17 +374,17 @@
             pltpu.VMEM(readout.shape, F32),
             pltpu.VMEM((3, 10, 8, 128), BF16),
             pltpu.VMEM((layers, 3, 4, 3, channels, 128), BF16),
-            pltpu.VMEM((8, 160, 256), BF16),
-            pltpu.VMEM((7, 160, 256), BF16),
-            pltpu.VMEM((2, 5, 160, 256), BF16),
-            pltpu.VMEM((2, 4, 160, 256), BF16),
-            pltpu.VMEM(events.shape, F32),
-            pltpu.VMEM(events.shape, F32),
+            pltpu.VMEM((10, 160, 256), BF16),
+            pltpu.VMEM((9, 160, 256), BF16),
+            pltpu.VMEM((2, 7, 160, 256), BF16),
+            pltpu.VMEM((2, 6, 160, 256), BF16),
+            pltpu.VMEM((lead + 1, *events.shape), F32),
             pltpu.SemaphoreType.DMA((7,)),
-            pltpu.SemaphoreType.DMA((6,)),
-            pltpu.SemaphoreType.DMA((6,)),
+            pltpu.SemaphoreType.DMA((6 + 2 * lead,)),
+            pltpu.SemaphoreType.DMA((6 + lead,)),
+            pltpu.SemaphoreType.REGULAR((lead + 1,)),
         ],
-        compiler_params=pltpu.CompilerParams(collective_id=0, has_side_effects=True, vmem_limit_bytes=48 * 1024 * 1024),
+        compiler_params=pltpu.CompilerParams(collective_id=0, has_side_effects=True, vmem_limit_bytes=67043328),
     )(events, soft_info, embed, gain, conv_weights, conv_bias, readout)
 
 

time: 62.9 us -> 41.6 us (0.66)
  the two profiles are of different devices: /device:TPU:65 before, /device:TPU:852 now
where the time goes in v2:
time: 41.6 us; the launch traced here: 41.3 us
  Pallas kernels  40 us (96%)
  local copies, waits for them, and re-layouts  1.32 us (3%)
    pallas_call x1, Pallas kernels, per_device(): pl.pallas_call(functools.partial(kernel, spaces, times, lead), out_shape=...  40 us
    unnamed x1, local copies, waits for them, and re-layouts  1.32 us

profile of v2, /device:TPU:852, one launch (start us, length us, event | category | flops | bytes accessed | tf_op | source)
XLA Modules:
  0.0 41.3 jit_solution(331839735245428146)
XLA Ops:
  0.0 40.0 %shard_map.73 = f32[4,8,128]{2,1,0:T(8,128)} custom-call(s32[4,8,128]{2,1,0:T(8,128)} %ev_hbm.1, bf16[4,8,128]{2,1,0:T(8,128)(2,1)} %so_hbm.1, f32[4,64]{1,0:T(4,128)} %emb_hbm.1, f32[1,64]{1,0:T(1,128)} %bitcast.2, bf16[3,64,1728]{2,1,0:T(8,128)(2,1)} %cw_hbm.1, f32[3,64]{1,0:T(4,128)} %cb_hbm.1, f32[1,64]{1,0:T(1,128)} %bitcast.3), custom_call_target="tpu_custom_call" | custom-call | tf_op jit(solution)/shard_map/pallas_call | solution.py:362
  40.0 1.3 %copy.9 = f32[4,8,128]{2,1,0:T(8,128)} copy(f32[4,8,128]{2,1,0:T(8,128)} %shard_map.73) | data formatting | bytes 32768

commit v3 on v2

--- a/solution.py
+++ b/solution.py
@@ -58,7 +58,7 @@
 
 def compute(
     spaces, space, time, up, down, later, earlier, barrier, grid_rows, remote, loads,
-    out_ref, ev, so, emb, gain, cw, cb, rw, win, unique, ha, hb, final, paired, result,
+    out_ref, ev, so, emb, gain, cw, cb, rw, win, unique, ha, hb, hc, ahead, final, paired, result,
 ):
     spread = one_hot(iota((128, 128), 0) == (iota((128, 128), 1) & 15) * 8 + (iota((128, 128), 1) >> 4))
     m = iota((64, 64), 0)
@@ -183,46 +183,37 @@
     pl.when(up)(to_below.wait_recv)
     pl.when(down)(to_above.wait_recv)
 
-    def first_kind(w, carry):
-        there = (w == 0) | later
-
-        @pl.when((w == 1) & later & up)
-        def _():
-            on_below.wait_recv()
-
-        @pl.when((w == 1) & later & down)
-        def _():
-            on_above.wait_recv()
-
+    pl.when(later & up)(on_below.wait_recv)
+    pl.when(later & down)(on_above.wait_recv)
+    for w, there in ((0, True), (1, later)):
         def cells(j, b):
             tile = win[2 * w, j].astype(F32)
             return tile[2 * b : 2 * b + 1], tile[2 * b + 1 : 2 * b + 2]
 
-        put(ha, (), start(cells, 10, base - 6, there), 10)
-        total = dot(jnp.concatenate(taps_of(ha, (), 0, 9), axis=1), within(0))
-        put(hb, (), finish(total, 0, 9, base - 5, there), 9)
-        total = dot(jnp.concatenate(taps_of(hb, (), 0, 8), axis=1), within(1))
-        put(ha, (), finish(total, 1, 8, base - 4, there), 8)
-        total = dot(jnp.concatenate(taps_of(ha, (), 0, 7), axis=1), within(2))
+        put(ha, (w,), start(cells, 10, base - 6, there), 10)
+    for w, there in ((0, True), (1, later)):
+        total = dot(jnp.concatenate(taps_of(ha, (w,), 0, 9), axis=1), within(0))
+        put(hb, (w,), finish(total, 0, 9, base - 5, there), 9)
+    for w, there in ((0, True), (1, later)):
+        total = dot(jnp.concatenate(taps_of(hb, (w,), 0, 8), axis=1), within(1))
+        put(hc, (w,), finish(total, 1, 8, base - 4, there), 8)
+    for w, there in ((0, True), (1, later)):
+        total = dot(jnp.concatenate(taps_of(hc, (w,), 0, 7), axis=1), within(2))
         value = finish(total, 2, 7, base - 3, there)
-        put(final, (w,), value, 7)
-        swapped = jnp.where((iota((6, 128, 256), 2) & 64) == 0, value[1:7], value[0:6])
-        put(
-            paired, (w,),
-            jnp.concatenate([pltpu.roll(swapped[:, :, :128], 64, 2), pltpu.roll(swapped[:, :, 128:], 64, 2)], axis=2),
-            6,
-        )
-        return carry
-
-    lax.fori_loop(0, 2, first_kind, 0)
+        half = 128 * w
+        put(final, (w,), value[:, :, half : half + 128], 7)
+        swapped = jnp.where((iota((6, 128, 128), 2) & 64) == 0, value[1:7, :, half : half + 128], value[0:6, :, half : half + 128])
+        put(paired, (w,), pltpu.roll(swapped, 64, 2), 6)
+        if w == 0:
+            ahead[...] = value[1:6, :, 128:256].astype(BF16)
 
     def beside(ref, first, count):
-        left = taps_of(ref.at[0, :, :, 0:128], (), first, count)
-        right = taps_of(ref.at[1, :, :, 128:256], (), first, count)
+        left = taps_of(ref, (0,), first, count)
+        right = taps_of(ref, (1,), first, count)
         return [v for pair in zip(left, right) for v in pair]
 
     def second(own, others, layer, count, first_other):
-        lhs = jnp.concatenate(taps_of(own, (), 0, count) + beside(others, first_other, count), axis=1)
+        lhs = jnp.concatenate(taps_of(own, (0,), 0, count) + beside(others, first_other, count), axis=1)
         return dot(lhs, jnp.concatenate([within(layer), across(layer)], axis=0))
 
     def late_cells(j, b):
@@ -230,16 +221,17 @@
         at = (b >> 1) * 4 + (1 - (b & 1)) * 2
         return tile[at : at + 1], tile[at + 1 : at + 2]
 
-    put(ha, (), start(late_cells, 7, base - 3, True), 7)
-    put(hb, (), finish(second(ha, final, 0, 6, 0), 0, 6, base - 2, True), 6)
-    put(ha, (), finish(second(hb, paired, 1, 5, 0), 1, 5, base - 1, True), 5)
-    last = finish(second(ha, final, 2, 4, 1), 2, 4, base, True).astype(BF16).reshape(512, 256)
+    put(ha, (0,), start(late_cells, 7, base - 3, True), 7)
+    put(hb, (0,), finish(second(ha, final, 0, 6, 0), 0, 6, base - 2, True), 6)
+    put(hc, (0,), finish(second(hb, paired, 1, 5, 0), 1, 5, base - 1, True), 5)
+    last = finish(second(hc, final, 2, 4, 1), 2, 4, base, True).astype(BF16).reshape(512, 256)
 
     w_terms = three_terms(quad(rw[...]))
     n = iota((32, 256), 0)
     weight = jnp.where(n >> 3 == 0, w_terms[0].astype(F32), jnp.where(n >> 3 == 1, w_terms[1].astype(F32), w_terms[2].astype(F32)))
     weight = jnp.where((n < 24) & ((n & 7) == iota((32, 256), 1) >> 6), weight, 0.0).astype(BF16)
-    a_sum = dot_nt(weight, final[0, 1:6, 16:144, :].reshape(640, 256))
+    first = jnp.concatenate([final[0, 1:6, 16:144, :].reshape(640, 128), ahead[...].reshape(640, 128)], axis=1)
+    a_sum = dot_nt(weight, first)
     b_sum = dot_nt(weight, last)
     a_sum = a_sum[0:8] + a_sum[8:16] + a_sum[16:24]
     b_sum = b_sum[0:8] + b_sum[8:16] + b_sum[16:24]
@@ -273,7 +265,7 @@
     ev_hbm, so_hbm, emb_hbm, gain_hbm, cw_hbm, cb_hbm, rw_hbm,
     out_ref,
     ev, so, emb, gain, cw, cb, rw,
-    win, unique, ha, hb, final, paired, result,
+    win, unique, ha, hb, hc, ahead, final, paired, result,
     load_sem, send_sem, recv_sem, hello,
 ):
     space, time, core = lax.axis_index("space"), lax.axis_index("tm"), lax.axis_index("chan")
@@ -333,7 +325,7 @@
 
         compute(
             spaces, space, time, up, down, later, earlier, barrier, grid_rows, remote, loads,
-            out_ref, ev, so, emb, gain, cw, cb, rw, win, unique, ha, hb, final, paired, result,
+            out_ref, ev, so, emb, gain, cw, cb, rw, win, unique, ha, hb, hc, ahead, final, paired, result,
         )
 
         passes = [remote(result.at[j], result.at[j + 1], 5 + j, 6 + j, {"space": space + 1}) for j in range(lead)]
@@ -374,18 +366,20 @@
             pltpu.VMEM(readout.shape, F32),
             pltpu.VMEM((3, 10, 8, 128), BF16),
             pltpu.VMEM((layers, 3, 4, 3, channels, 128), BF16),
-            pltpu.VMEM((10, 160, 256), BF16),
-            pltpu.VMEM((9, 160, 256), BF16),
-            pltpu.VMEM((2, 7, 160, 256), BF16),
-            pltpu.VMEM((2, 6, 160, 256), BF16),
+            pltpu.VMEM((2, 10, 160, 256), BF16),
+            pltpu.VMEM((2, 9, 160, 256), BF16),
+            pltpu.VMEM((2, 8, 160, 256), BF16),
+            pltpu.VMEM((5, 128, 128), BF16),
+            pltpu.VMEM((2, 7, 160, 128), BF16),
+            pltpu.VMEM((2, 6, 160, 128), BF16),
             pltpu.VMEM((lead + 1, *events.shape), F32),
             pltpu.SemaphoreType.DMA((7,)),
             pltpu.SemaphoreType.DMA((6 + 2 * lead,)),
             pltpu.SemaphoreType.DMA((6 + lead,)),
             pltpu.SemaphoreType.REGULAR((lead + 1,)),
         ],
-        compiler_params=pltpu.CompilerParams(collective_id=0, has_side_effects=True, vmem_limit_bytes=67043328),
-    )(events, soft_info, embed, gain, conv_weights, conv_bias, readout)
+        compiler_params=pltpu.CompilerParams(collective_id=0, has_side_effects=True, vmem_limit_bytes=48 * 1024 * 1024),
+    )(*[pltpu.with_memory_space_constraint(v, pltpu.HBM) for v in (events, soft_info, embed, gain, conv_weights, conv_bias, readout)])
 
 
 def solution(mesh):

time: 41.6 us -> 40.9 us (0.983)
  the two profiles are of different devices: /device:TPU:852 before, /device:TPU:838 now
where the time goes in v3:
time: 40.9 us; the launch traced here: 40.7 us
  Pallas kernels  40.1 us (98%)
  local copies, waits for them, and re-layouts  0.61 us (1%)
    pallas_call x1, Pallas kernels, per_device(): pl.pallas_call(functools.partial(kernel, spaces, times, lead), out_shape=...  40.1 us

profile of v3, /device:TPU:838, one launch (start us, length us, event | category | flops | bytes accessed | tf_op | source)
XLA Modules:
  0.0 40.7 jit_solution(8897741296021102207)
XLA Ops:
  0.0 40.1 %shard_map.73 = f32[4,8,128]{2,1,0:T(8,128)S(1)} custom-call(s32[4,8,128]{2,1,0:T(8,128)} %ev_hbm.1, bf16[4,8,128]{2,1,0:T(8,128)(2,1)} %so_hbm.1, f32[4,64]{1,0:T(4,128)} %emb_hbm.1, f32[1,64]{1,0:T(1,128)} %bitcast.2, bf16[3,64,1728]{2,1,0:T(8,128)(2,1)} %cw_hbm.1, f32[3,64]{1,0:T(4,128)} %cb_hbm.1, f32[1,64]{1,0:T(1,128)} %bitcast.3), custom_call_target="tpu_custom_call" | custom-call | tf_op jit(solution)/shard_map/pallas_call | solution.py:354
  40.1 0.6 %copy.9 = f32[4,8,128]{2,1,0:T(8,128)} copy(f32[4,8,128]{2,1,0:T(8,128)S(1)} %shard_map.73) | data formatting | bytes 32768

commit v4 on v3

--- a/solution.py
+++ b/solution.py
@@ -10,7 +10,7 @@
 F32 = jnp.float32
 BF16 = jnp.bfloat16
 MESH = pl.DeviceIdType.MESH
-LEAD = 3
+LEAD = 4
 
 
 def iota(shape, dim):
@@ -45,19 +45,19 @@
     return jnp.concatenate([row] * 4, axis=1)
 
 
-def put(ref, lead, value, count):
+def put(ref, lead, value, first, count):
     width = value.shape[2]
     q = iota((count, 16, width), 1)
-    last, first = value[:, 112:128], value[:, 0:16]
+    last, head = value[:, 112:128], value[:, 0:16]
     before = jnp.where(q == 0, 0.0, pltpu.roll(last, 1, 1))
-    after = jnp.where(q == 15, 0.0, pltpu.roll(first, 15, 1))
-    ref[(*lead, pl.ds(0, count), pl.ds(0, 16))] = before.astype(BF16)
-    ref[(*lead, pl.ds(0, count), pl.ds(16, 128))] = value.astype(BF16)
-    ref[(*lead, pl.ds(0, count), pl.ds(144, 16))] = after.astype(BF16)
+    after = jnp.where(q == 15, 0.0, pltpu.roll(head, 15, 1))
+    ref[(*lead, pl.ds(first, count), pl.ds(0, 16))] = before.astype(BF16)
+    ref[(*lead, pl.ds(first, count), pl.ds(16, 128))] = value.astype(BF16)
+    ref[(*lead, pl.ds(first, count), pl.ds(144, 16))] = after.astype(BF16)
 
 
 def compute(
-    spaces, space, time, up, down, later, earlier, barrier, grid_rows, remote, loads,
+    spaces, space, time, up, down, later, earlier, barrier, ready, grid_rows, remote, loads,
     out_ref, ev, so, emb, gain, cw, cb, rw, win, unique, ha, hb, hc, ahead, final, paired, result,
 ):
     spread = one_hot(iota((128, 128), 0) == (iota((128, 128), 1) & 15) * 8 + (iota((128, 128), 1) >> 4))
@@ -77,15 +77,19 @@
     to_above = remote(win.at[0:2, 3:6], win.at[0:2, 7:10], 1, 1, {"space": space - 1})
     to_earlier = remote(win.at[0, 3:7], win.at[2, 3:7], 2, 2, {"tm": time - 1})
     on_below = remote(win.at[2, 4:7], win.at[2, 0:3], 3, 3, {"space": space + 1})
-    on_above = remote(win.at[2, 3:6], win.at[2, 7:10], 4, 4, {"space": space - 1})
+    to_corner = remote(win.at[0, 3:6], win.at[2, 7:10], 4, 4, {"space": space - 1, "tm": time - 1})
 
     pl.semaphore_wait(
         barrier,
-        jnp.where(up, 1, 0) + jnp.where(down, 1, 0) + jnp.where(later, 1, 0) + jnp.where(earlier, 1, 0),
+        jnp.where(up, 1, 0) + jnp.where(later, 1, 0) + jnp.where(earlier, 1, 0) + jnp.where(up & earlier, 1, 0),
     )
-    pl.when(down)(to_below.start)
     pl.when(up)(to_above.start)
+    pl.when(up & earlier)(to_corner.start)
     pl.when(earlier)(to_earlier.start)
+
+    @pl.when(up)
+    def _():
+        pl.semaphore_signal(ready, inc=1, device_id={"space": space - 1}, device_id_type=MESH)
 
     loads[2].wait()
     blank = jnp.zeros((3, 1, 3, 16, 128), F32)
@@ -130,9 +134,9 @@
         value = jnp.where(k < 12, jnp.where(code == (k & 3), 1.0, 0.0), jnp.where(k < 15, signal, 0.0))
         return jnp.where(inside, value, 0.0)
 
-    def start(cells, count, first_row, there):
+    def start(cells, first, count, first_row, there):
         columns = []
-        for j in range(count):
+        for j in range(first, first + count):
             blocks = []
             for b in range(4):
                 blocks.append(inputs(cells(j, b), first_row + 2 * j + (b & 1), there))
@@ -177,33 +181,51 @@
         value = jnp.maximum(total + bias[layer], 0.0).reshape(count, 128, 256)
         return value * jnp.where(inside, 1.0, 0.0)
 
-    pl.when(later)(to_earlier.wait_recv)
-    pl.when(later & down)(on_below.start)
-    pl.when(later & up)(on_above.start)
-    pl.when(up)(to_below.wait_recv)
-    pl.when(down)(to_above.wait_recv)
-
-    pl.when(later & up)(on_below.wait_recv)
-    pl.when(later & down)(on_above.wait_recv)
-    for w, there in ((0, True), (1, later)):
+    windows = ((0, True), (1, later))
+
+    def begin(w, there, first, count):
         def cells(j, b):
             tile = win[2 * w, j].astype(F32)
             return tile[2 * b : 2 * b + 1], tile[2 * b + 1 : 2 * b + 2]
 
-        put(ha, (w,), start(cells, 10, base - 6, there), 10)
-    for w, there in ((0, True), (1, later)):
-        total = dot(jnp.concatenate(taps_of(ha, (w,), 0, 9), axis=1), within(0))
-        put(hb, (w,), finish(total, 0, 9, base - 5, there), 9)
+        put(ha, (w,), start(cells, first, count, base - 6, there), first, count)
+
+    def first_layer(w, there, first, count):
+        total = dot(jnp.concatenate(taps_of(ha, (w,), first, count), axis=1), within(0))
+        put(hb, (w,), finish(total, 0, count, base - 5 + 2 * first, there), first, count)
+
+    pl.when(later)(to_earlier.wait_recv)
+    for w, there in windows:
+        begin(w, there, 3, 4)
+
+    @pl.when(down)
+    def _():
+        pl.semaphore_wait(ready, 1)
+        to_below.start()
+
+    pl.when(down & later)(on_below.start)
+    pl.when(up)(to_below.wait_recv)
+    pl.when(up & later)(on_below.wait_recv)
+    for w, there in windows:
+        begin(w, there, 0, 3)
+    for w, there in windows:
+        first_layer(w, there, 0, 6)
+    pl.when(down)(to_above.wait_recv)
+    pl.when(down & later)(to_corner.wait_recv)
+    for w, there in windows:
+        begin(w, there, 7, 3)
+    for w, there in windows:
+        first_layer(w, there, 6, 3)
     for w, there in ((0, True), (1, later)):
         total = dot(jnp.concatenate(taps_of(hb, (w,), 0, 8), axis=1), within(1))
-        put(hc, (w,), finish(total, 1, 8, base - 4, there), 8)
+        put(hc, (w,), finish(total, 1, 8, base - 4, there), 0, 8)
     for w, there in ((0, True), (1, later)):
         total = dot(jnp.concatenate(taps_of(hc, (w,), 0, 7), axis=1), within(2))
         value = finish(total, 2, 7, base - 3, there)
         half = 128 * w
-        put(final, (w,), value[:, :, half : half + 128], 7)
+        put(final, (w,), value[:, :, half : half + 128], 0, 7)
         swapped = jnp.where((iota((6, 128, 128), 2) & 64) == 0, value[1:7, :, half : half + 128], value[0:6, :, half : half + 128])
-        put(paired, (w,), pltpu.roll(swapped, 64, 2), 6)
+        put(paired, (w,), pltpu.roll(swapped, 64, 2), 0, 6)
         if w == 0:
             ahead[...] = value[1:6, :, 128:256].astype(BF16)
 
@@ -221,9 +243,9 @@
         at = (b >> 1) * 4 + (1 - (b & 1)) * 2
         return tile[at : at + 1], tile[at + 1 : at + 2]
 
-    put(ha, (0,), start(late_cells, 7, base - 3, True), 7)
-    put(hb, (0,), finish(second(ha, final, 0, 6, 0), 0, 6, base - 2, True), 6)
-    put(hc, (0,), finish(second(hb, paired, 1, 5, 0), 1, 5, base - 1, True), 5)
+    put(ha, (0,), start(late_cells, 0, 7, base - 3, True), 0, 7)
+    put(hb, (0,), finish(second(ha, final, 0, 6, 0), 0, 6, base - 2, True), 0, 6)
+    put(hc, (0,), finish(second(hb, paired, 1, 5, 0), 1, 5, base - 1, True), 0, 5)
     last = finish(second(hc, final, 2, 4, 1), 2, 4, base, True).astype(BF16).reshape(512, 256)
 
     w_terms = three_terms(quad(rw[...]))
@@ -257,7 +279,7 @@
     pl.when(up)(to_above.wait_send)
     pl.when(earlier)(to_earlier.wait_send)
     pl.when(later & down)(on_below.wait_send)
-    pl.when(later & up)(on_above.wait_send)
+    pl.when(up & earlier)(to_corner.wait_send)
 
 
 def kernel(
@@ -266,7 +288,7 @@
     out_ref,
     ev, so, emb, gain, cw, cb, rw,
     win, unique, ha, hb, hc, ahead, final, paired, result,
-    load_sem, send_sem, recv_sem, hello,
+    load_sem, send_sem, recv_sem, hello, ready,
 ):
     space, time, core = lax.axis_index("space"), lax.axis_index("tm"), lax.axis_index("chan")
     worker = core == lax.axis_size("chan") - 1
@@ -316,15 +338,15 @@
             def _():
                 pl.semaphore_signal(barrier, inc=1, device_id=device, device_id_type=MESH)
 
-        greet(up, {"space": space - 1})
         greet(down, {"space": space + 1})
         greet(later, {"tm": time + 1})
         greet(earlier, {"tm": time - 1})
+        greet(down & later, {"space": space + 1, "tm": time + 1})
         for j in range(lead + 1):
             greet(serves(j), {"space": space - j, "chan": core - 1})
 
         compute(
-            spaces, space, time, up, down, later, earlier, barrier, grid_rows, remote, loads,
+            spaces, space, time, up, down, later, earlier, barrier, ready, grid_rows, remote, loads,
             out_ref, ev, so, emb, gain, cw, cb, rw, win, unique, ha, hb, hc, ahead, final, paired, result,
         )
 
@@ -377,6 +399,7 @@
             pltpu.SemaphoreType.DMA((6 + 2 * lead,)),
             pltpu.SemaphoreType.DMA((6 + lead,)),
             pltpu.SemaphoreType.REGULAR((lead + 1,)),
+            pltpu.SemaphoreType.REGULAR,
         ],
         compiler_params=pltpu.CompilerParams(collective_id=0, has_side_effects=True, vmem_limit_bytes=48 * 1024 * 1024),
     )(*[pltpu.with_memory_space_constraint(v, pltpu.HBM) for v in (events, soft_info, embed, gain, conv_weights, conv_bias, readout)])

time: 40.9 us -> 39.4 us (0.963)
  the two profiles are of different devices: /device:TPU:838 before, /device:TPU:852 now
where the time goes in v4:
time: 39.4 us; the launch traced here: 39.3 us
  Pallas kernels  38.6 us (98%)
  local copies, waits for them, and re-layouts  0.61 us (2%)
    pallas_call x1, Pallas kernels, per_device(): pl.pallas_call(functools.partial(kernel, spaces, times, lead), out_shape=...  38.6 us

profile of v4, /device:TPU:852, one launch (start us, length us, event | category | flops | bytes accessed | tf_op | source)
XLA Modules:
  0.0 39.3 jit_solution(5636039658445186575)
XLA Ops:
  0.0 38.6 %shard_map.73 = f32[4,8,128]{2,1,0:T(8,128)S(1)} custom-call(s32[4,8,128]{2,1,0:T(8,128)} %ev_hbm.1, bf16[4,8,128]{2,1,0:T(8,128)(2,1)} %so_hbm.1, f32[4,64]{1,0:T(4,128)} %emb_hbm.1, f32[1,64]{1,0:T(1,128)} %bitcast.2, bf16[3,64,1728]{2,1,0:T(8,128)(2,1)} %cw_hbm.1, f32[3,64]{1,0:T(4,128)} %cb_hbm.1, f32[1,64]{1,0:T(1,128)} %bitcast.3), custom_call_target="tpu_custom_call" | custom-call | tf_op jit(solution)/shard_map/pallas_call | solution.py:376
  38.7 0.6 %copy.9 = f32[4,8,128]{2,1,0:T(8,128)} copy(f32[4,8,128]{2,1,0:T(8,128)S(1)} %shard_map.73) | data formatting | bytes 32768

commit v5 on v4

--- a/solution.py
+++ b/solution.py
@@ -10,7 +10,7 @@
 F32 = jnp.float32
 BF16 = jnp.bfloat16
 MESH = pl.DeviceIdType.MESH
-LEAD = 4
+LEAD = 3
 
 
 def iota(shape, dim):
@@ -58,7 +58,7 @@
 
 def compute(
     spaces, space, time, up, down, later, earlier, barrier, ready, grid_rows, remote, loads,
-    out_ref, ev, so, emb, gain, cw, cb, rw, win, unique, ha, hb, hc, ahead, final, paired, result,
+    out_ref, ev, so, emb, gain, cw, cb, rw, win, unique, ha, hb, hc, hd, ahead, final, paired, result,
 ):
     spread = one_hot(iota((128, 128), 0) == (iota((128, 128), 1) & 15) * 8 + (iota((128, 128), 1) >> 4))
     m = iota((64, 64), 0)
@@ -181,6 +181,11 @@
         value = jnp.maximum(total + bias[layer], 0.0).reshape(count, 128, 256)
         return value * jnp.where(inside, 1.0, 0.0)
 
+    def late_cells(j, b):
+        tile = win[1, 1 + j + (b & 1)].astype(F32)
+        at = (b >> 1) * 4 + (1 - (b & 1)) * 2
+        return tile[at : at + 1], tile[at + 1 : at + 2]
+
     windows = ((0, True), (1, later))
 
     def begin(w, there, first, count):
@@ -193,6 +198,22 @@
     def first_layer(w, there, first, count):
         total = dot(jnp.concatenate(taps_of(ha, (w,), first, count), axis=1), within(0))
         put(hb, (w,), finish(total, 0, count, base - 5 + 2 * first, there), first, count)
+
+    def middle_layer(w, there, first, count):
+        total = dot(jnp.concatenate(taps_of(hb, (w,), first, count), axis=1), within(1))
+        put(hc, (w,), finish(total, 1, count, base - 4 + 2 * first, there), first, count)
+
+    def last_layer(w, there, first, count):
+        total = dot(jnp.concatenate(taps_of(hc, (w,), first, count), axis=1), within(2))
+        value = finish(total, 2, count, base - 3 + 2 * first, there)
+        put(final, (w,), value[:, :, 128 * w : 128 * w + 128], first, count)
+        if w == 0:
+            ahead[first : first + count] = value[:, :, 128:256].astype(BF16)
+
+    def pair_again(w, first, count):
+        one, two = final[w, first : first + count].astype(F32), final[w, first + 1 : first + 1 + count].astype(F32)
+        swapped = jnp.where(iota((count, 160, 128), 2) < 64, two, one)
+        paired[w, first : first + count] = pltpu.roll(swapped, 64, 2).astype(BF16)
 
     pl.when(later)(to_earlier.wait_recv)
     for w, there in windows:
@@ -208,26 +229,22 @@
     pl.when(up & later)(on_below.wait_recv)
     for w, there in windows:
         begin(w, there, 0, 3)
-    for w, there in windows:
-        first_layer(w, there, 0, 6)
+    for layer, count in ((first_layer, 6), (middle_layer, 5), (last_layer, 4)):
+        for w, there in windows:
+            layer(w, there, 0, count)
+    put(hd, (0,), start(late_cells, 0, 5, base - 3, True), 0, 5)
+    for w in range(2):
+        pair_again(w, 0, 3)
     pl.when(down)(to_above.wait_recv)
     pl.when(down & later)(to_corner.wait_recv)
     for w, there in windows:
         begin(w, there, 7, 3)
-    for w, there in windows:
-        first_layer(w, there, 6, 3)
-    for w, there in ((0, True), (1, later)):
-        total = dot(jnp.concatenate(taps_of(hb, (w,), 0, 8), axis=1), within(1))
-        put(hc, (w,), finish(total, 1, 8, base - 4, there), 0, 8)
-    for w, there in ((0, True), (1, later)):
-        total = dot(jnp.concatenate(taps_of(hc, (w,), 0, 7), axis=1), within(2))
-        value = finish(total, 2, 7, base - 3, there)
-        half = 128 * w
-        put(final, (w,), value[:, :, half : half + 128], 0, 7)
-        swapped = jnp.where((iota((6, 128, 128), 2) & 64) == 0, value[1:7, :, half : half + 128], value[0:6, :, half : half + 128])
-        put(paired, (w,), pltpu.roll(swapped, 64, 2), 0, 6)
-        if w == 0:
-            ahead[...] = value[1:6, :, 128:256].astype(BF16)
+    for layer, first in ((first_layer, 6), (middle_layer, 5), (last_layer, 4)):
+        for w, there in windows:
+            layer(w, there, first, 3)
+    put(hd, (0,), start(late_cells, 5, 2, base - 3, True), 5, 2)
+    for w in range(2):
+        pair_again(w, 3, 3)
 
     def beside(ref, first, count):
         left = taps_of(ref, (0,), first, count)
@@ -238,13 +255,7 @@
         lhs = jnp.concatenate(taps_of(own, (0,), 0, count) + beside(others, first_other, count), axis=1)
         return dot(lhs, jnp.concatenate([within(layer), across(layer)], axis=0))
 
-    def late_cells(j, b):
-        tile = win[1, 1 + j + (b & 1)].astype(F32)
-        at = (b >> 1) * 4 + (1 - (b & 1)) * 2
-        return tile[at : at + 1], tile[at + 1 : at + 2]
-
-    put(ha, (0,), start(late_cells, 0, 7, base - 3, True), 0, 7)
-    put(hb, (0,), finish(second(ha, final, 0, 6, 0), 0, 6, base - 2, True), 0, 6)
+    put(hb, (0,), finish(second(hd, final, 0, 6, 0), 0, 6, base - 2, True), 0, 6)
     put(hc, (0,), finish(second(hb, paired, 1, 5, 0), 1, 5, base - 1, True), 0, 5)
     last = finish(second(hc, final, 2, 4, 1), 2, 4, base, True).astype(BF16).reshape(512, 256)
 
@@ -252,7 +263,7 @@
     n = iota((32, 256), 0)
     weight = jnp.where(n >> 3 == 0, w_terms[0].astype(F32), jnp.where(n >> 3 == 1, w_terms[1].astype(F32), w_terms[2].astype(F32)))
     weight = jnp.where((n < 24) & ((n & 7) == iota((32, 256), 1) >> 6), weight, 0.0).astype(BF16)
-    first = jnp.concatenate([final[0, 1:6, 16:144, :].reshape(640, 128), ahead[...].reshape(640, 128)], axis=1)
+    first = jnp.concatenate([final[0, 1:6, 16:144, :].reshape(640, 128), ahead[1:6].reshape(640, 128)], axis=1)
     a_sum = dot_nt(weight, first)
     b_sum = dot_nt(weight, last)
     a_sum = a_sum[0:8] + a_sum[8:16] + a_sum[16:24]
@@ -287,7 +298,7 @@
     ev_hbm, so_hbm, emb_hbm, gain_hbm, cw_hbm, cb_hbm, rw_hbm,
     out_ref,
     ev, so, emb, gain, cw, cb, rw,
-    win, unique, ha, hb, hc, ahead, final, paired, result,
+    win, unique, ha, hb, hc, hd, ahead, final, paired, result,
     load_sem, send_sem, recv_sem, hello, ready,
 ):
     space, time, core = lax.axis_index("space"), lax.axis_index("tm"), lax.axis_index("chan")
@@ -347,7 +358,7 @@
 
         compute(
             spaces, space, time, up, down, later, earlier, barrier, ready, grid_rows, remote, loads,
-            out_ref, ev, so, emb, gain, cw, cb, rw, win, unique, ha, hb, hc, ahead, final, paired, result,
+            out_ref, ev, so, emb, gain, cw, cb, rw, win, unique, ha, hb, hc, hd, ahead, final, paired, result,
         )
 
         passes = [remote(result.at[j], result.at[j + 1], 5 + j, 6 + j, {"space": space + 1}) for j in range(lead)]
@@ -391,7 +402,8 @@
             pltpu.VMEM((2, 10, 160, 256), BF16),
             pltpu.VMEM((2, 9, 160, 256), BF16),
             pltpu.VMEM((2, 8, 160, 256), BF16),
-            pltpu.VMEM((5, 128, 128), BF16),
+            pltpu.VMEM((1, 7, 160, 256), BF16),
+            pltpu.VMEM((7, 128, 128), BF16),
             pltpu.VMEM((2, 7, 160, 128), BF16),
             pltpu.VMEM((2, 6, 160, 128), BF16),
             pltpu.VMEM((lead + 1, *events.shape), F32),

time: 39.4 us -> 35.6 us (0.904)
  the two profiles are of different devices: /device:TPU:852 before, /device:TPU:833 now
where the time goes in v5:
time: 35.6 us; the launch traced here: 35.4 us
  Pallas kernels  34.8 us (98%)
  local copies, waits for them, and re-layouts  0.61 us (2%)
    pallas_call x1, Pallas kernels, per_device(): pl.pallas_call(functools.partial(kernel, spaces, times, lead), out_shape=...  34.8 us

profile of v5, /device:TPU:833, one launch (start us, length us, event | category | flops | bytes accessed | tf_op | source)
XLA Modules:
  0.0 35.4 jit_solution(10555253420454980813)
XLA Ops:
  0.0 34.8 %shard_map.73 = f32[4,8,128]{2,1,0:T(8,128)S(1)} custom-call(s32[4,8,128]{2,1,0:T(8,128)} %ev_hbm.1, bf16[4,8,128]{2,1,0:T(8,128)(2,1)} %so_hbm.1, f32[4,64]{1,0:T(4,128)} %emb_hbm.1, f32[1,64]{1,0:T(1,128)} %bitcast.2, bf16[3,64,1728]{2,1,0:T(8,128)(2,1)} %cw_hbm.1, f32[3,64]{1,0:T(4,128)} %cb_hbm.1, f32[1,64]{1,0:T(1,128)} %bitcast.3), custom_call_target="tpu_custom_call" | custom-call | tf_op jit(solution)/shard_map/pallas_call | solution.py:387
  34.8 0.6 %copy.9 = f32[4,8,128]{2,1,0:T(8,128)} copy(f32[4,8,128]{2,1,0:T(8,128)S(1)} %shard_map.73) | data formatting | bytes 32768

commit v6 on v5

--- a/solution.py
+++ b/solution.py
@@ -10,7 +10,7 @@
 F32 = jnp.float32
 BF16 = jnp.bfloat16
 MESH = pl.DeviceIdType.MESH
-LEAD = 3
+LEAD = 5
 
 
 def iota(shape, dim):
@@ -57,7 +57,7 @@
 
 
 def compute(
-    spaces, space, time, up, down, later, earlier, barrier, ready, grid_rows, remote, loads,
+    spaces, space, time, near, up, down, later, earlier, barrier, ready, grid_rows, remote, loads,
     out_ref, ev, so, emb, gain, cw, cb, rw, win, unique, ha, hb, hc, hd, ahead, final, paired, result,
 ):
     spread = one_hot(iota((128, 128), 0) == (iota((128, 128), 1) & 15) * 8 + (iota((128, 128), 1) >> 4))
@@ -81,7 +81,8 @@
 
     pl.semaphore_wait(
         barrier,
-        jnp.where(up, 1, 0) + jnp.where(later, 1, 0) + jnp.where(earlier, 1, 0) + jnp.where(up & earlier, 1, 0),
+        jnp.where(up, 1, 0) + jnp.where(later, 1, 0) + jnp.where(earlier, 1, 0) + jnp.where(up & earlier, 1, 0)
+        + jnp.where(near, 1, 0),
     )
     pl.when(up)(to_above.start)
     pl.when(up & earlier)(to_corner.start)
@@ -299,7 +300,7 @@
     out_ref,
     ev, so, emb, gain, cw, cb, rw,
     win, unique, ha, hb, hc, hd, ahead, final, paired, result,
-    load_sem, send_sem, recv_sem, hello, ready,
+    load_sem, send_sem, recv_sem, hello, taker, ready,
 ):
     space, time, core = lax.axis_index("space"), lax.axis_index("tm"), lax.axis_index("chan")
     worker = core == lax.axis_size("chan") - 1
@@ -314,24 +315,39 @@
             device_id=device, device_id_type=MESH,
         )
 
-    def serves(j):
-        return space >= j if j == lead else (space >= j) & (space == spaces - 1)
-
-    gives = [
-        remote(result.at[j], result.at[0], 5 + lead + j, 5, {"space": space - j, "chan": core - 1}) for j in range(lead + 1)
-    ]
+    first = space == 0 if lead > 0 else space < 0
+    keeper = space == lead if lead > 0 else space < 0
+    near = jnp.logical_not(first)
+    give = remote(result.at[0], result.at[0], 5, 5, {"chan": core - 1})
+    keep = remote(result.at[0], result.at[1], 6, 6, {"space": space + lead, "chan": core - 1})
+    serve = remote(result.at[1], result.at[0], 7, 5, {"space": space - lead})
+
+    def signal(there, semaphore, device):
+        @pl.when(there)
+        def _():
+            pl.semaphore_signal(semaphore, inc=1, device_id=device, device_id_type=MESH)
 
     @pl.when(jnp.logical_not(worker))
     def _():
-        pl.semaphore_wait(barrier, 1)
-        for j in range(lead + 1):
-            @pl.when(space + lead <= spaces - 1 if j == lead else space == spaces - 1 - j)
-            def _():
-                pl.semaphore_signal(
-                    hello.at[j], inc=1, device_id={"space": space + j, "chan": core + 1}, device_id_type=MESH
-                )
-        gives[0].wait_recv()
+        signal(near, barrier, {"chan": core + 1})
+        signal(keeper, barrier, {"space": space - lead})
+
+        @pl.when(first | keeper)
+        def _():
+            pl.semaphore_wait(barrier, 1)
+
+        signal(first, hello, {"space": space + lead})
+        signal(keeper, taker, {"space": space - lead, "chan": core + 1})
+
+        @pl.when(keeper)
+        def _():
+            keep.wait_recv()
+            pl.semaphore_wait(hello, 1)
+            serve.start()
+
+        give.wait_recv()
         out_ref[...] = result[0]
+        pl.when(keeper)(serve.wait_send)
 
     @pl.when(worker)
     def _():
@@ -344,38 +360,25 @@
         for load in loads:
             load.start()
 
-        def greet(there, device):
-            @pl.when(there)
-            def _():
-                pl.semaphore_signal(barrier, inc=1, device_id=device, device_id_type=MESH)
-
-        greet(down, {"space": space + 1})
-        greet(later, {"tm": time + 1})
-        greet(earlier, {"tm": time - 1})
-        greet(down & later, {"space": space + 1, "tm": time + 1})
-        for j in range(lead + 1):
-            greet(serves(j), {"space": space - j, "chan": core - 1})
-
+        signal(first, barrier, {"space": space + lead, "chan": core - 1})
+        signal(down, barrier, {"space": space + 1})
+        signal(later, barrier, {"tm": time + 1})
+        signal(earlier, barrier, {"tm": time - 1})
+        signal(down & later, barrier, {"space": space + 1, "tm": time + 1})
         compute(
-            spaces, space, time, up, down, later, earlier, barrier, ready, grid_rows, remote, loads,
+            spaces, space, time, near, up, down, later, earlier, barrier, ready, grid_rows, remote, loads,
             out_ref, ev, so, emb, gain, cw, cb, rw, win, unique, ha, hb, hc, hd, ahead, final, paired, result,
         )
 
-        passes = [remote(result.at[j], result.at[j + 1], 5 + j, 6 + j, {"space": space + 1}) for j in range(lead)]
-        for j in range(lead + 1):
-            if j > 0:
-                pl.when(space >= j)(passes[j - 1].wait_recv)
-            if j < lead:
-                pl.when(down & (space >= j))(passes[j].start)
-        for j in range(lead + 1):
-            @pl.when(serves(j))
-            def _():
-                pl.semaphore_wait(hello.at[j], 1)
-                gives[j].start()
-        for j in range(lead):
-            pl.when(down & (space >= j))(passes[j].wait_send)
-        for j in range(lead + 1):
-            pl.when(serves(j))(gives[j].wait_send)
+        pl.when(near)(give.start)
+
+        @pl.when(first)
+        def _():
+            pl.semaphore_wait(taker, 1)
+            keep.start()
+
+        pl.when(near)(give.wait_send)
+        pl.when(first)(keep.wait_send)
 
 
 def per_device(spaces, times, events, soft_info, embed, soft_gain, conv_weights, conv_bias, readout_weight):
@@ -406,11 +409,12 @@
             pltpu.VMEM((7, 128, 128), BF16),
             pltpu.VMEM((2, 7, 160, 128), BF16),
             pltpu.VMEM((2, 6, 160, 128), BF16),
-            pltpu.VMEM((lead + 1, *events.shape), F32),
+            pltpu.VMEM((2, *events.shape), F32),
             pltpu.SemaphoreType.DMA((7,)),
-            pltpu.SemaphoreType.DMA((6 + 2 * lead,)),
-            pltpu.SemaphoreType.DMA((6 + lead,)),
-            pltpu.SemaphoreType.REGULAR((lead + 1,)),
+            pltpu.SemaphoreType.DMA((8,)),
+            pltpu.SemaphoreType.DMA((7,)),
+            pltpu.SemaphoreType.REGULAR,
+            pltpu.SemaphoreType.REGULAR,
             pltpu.SemaphoreType.REGULAR,
         ],
         compiler_params=pltpu.CompilerParams(collective_id=0, has_side_effects=True, vmem_limit_bytes=48 * 1024 * 1024),

time: 35.6 us -> 30.9 us (0.87)
  the two profiles are of different devices: /device:TPU:833 before, /device:TPU:88 now
where the time goes in v6:
time: 30.9 us; the launch traced here: 30.7 us
  Pallas kernels  30.1 us (97%)
  local copies, waits for them, and re-layouts  0.61 us (2%)
    pallas_call x1, Pallas kernels, per_device(): pl.pallas_call(functools.partial(kernel, spaces, times, lead), out_shape=...  30.1 us

profile of v6, /device:TPU:88, one launch (start us, length us, event | category | flops | bytes accessed | tf_op | source)
XLA Modules:
  0.0 30.7 jit_solution(8797327003961936318)
XLA Ops:
  0.0 30.1 %shard_map.73 = f32[4,8,128]{2,1,0:T(8,128)S(1)} custom-call(s32[4,8,128]{2,1,0:T(8,128)} %ev_hbm.1, bf16[4,8,128]{2,1,0:T(8,128)(2,1)} %so_hbm.1, f32[4,64]{1,0:T(4,128)} %emb_hbm.1, f32[1,64]{1,0:T(1,128)} %bitcast.2, bf16[3,64,1728]{2,1,0:T(8,128)(2,1)} %cw_hbm.1, f32[3,64]{1,0:T(4,128)} %cb_hbm.1, f32[1,64]{1,0:T(1,128)} %bitcast.3), custom_call_target="tpu_custom_call" | custom-call | tf_op jit(solution)/shard_map/pallas_call | solution.py:390
  30.1 0.6 %copy.9 = f32[4,8,128]{2,1,0:T(8,128)} copy(f32[4,8,128]{2,1,0:T(8,128)S(1)} %shard_map.73) | data formatting | bytes 32768

commit v7 on v6

--- a/solution.py
+++ b/solution.py
@@ -10,7 +10,7 @@
 F32 = jnp.float32
 BF16 = jnp.bfloat16
 MESH = pl.DeviceIdType.MESH
-LEAD = 5
+LEAD = 4, 6
 
 
 def iota(shape, dim):
@@ -315,12 +315,16 @@
             device_id=device, device_id_type=MESH,
         )
 
-    first = space == 0 if lead > 0 else space < 0
-    keeper = space == lead if lead > 0 else space < 0
+    halfway, whole = lead
+    far = whole > 1
+    first = space == 0 if far else space < 0
+    relay = space == halfway if far else space < 0
+    keeper = space == whole if far else space < 0
     near = jnp.logical_not(first)
     give = remote(result.at[0], result.at[0], 5, 5, {"chan": core - 1})
-    keep = remote(result.at[0], result.at[1], 6, 6, {"space": space + lead, "chan": core - 1})
-    serve = remote(result.at[1], result.at[0], 7, 5, {"space": space - lead})
+    keep = remote(result.at[0], result.at[1], 6, 6, {"space": space + halfway, "chan": core - 1})
+    pass_on = remote(result.at[1], result.at[1], 7, 6, {"space": space + whole - halfway})
+    serve = remote(result.at[1], result.at[0], 7, 5, {"space": space - whole})
 
     def signal(there, semaphore, device):
         @pl.when(there)
@@ -330,23 +334,32 @@
     @pl.when(jnp.logical_not(worker))
     def _():
         signal(near, barrier, {"chan": core + 1})
-        signal(keeper, barrier, {"space": space - lead})
-
-        @pl.when(first | keeper)
+        signal(relay, barrier, {"space": space + whole - halfway})
+        signal(keeper, barrier, {"space": space - whole})
+
+        @pl.when(first | relay | keeper)
         def _():
             pl.semaphore_wait(barrier, 1)
 
-        signal(first, hello, {"space": space + lead})
-        signal(keeper, taker, {"space": space - lead, "chan": core + 1})
+        signal(first, hello, {"space": space + whole})
+        signal(relay, taker, {"space": space - halfway, "chan": core + 1})
+        signal(keeper, taker, {"space": space + halfway - whole})
+
+        @pl.when(relay)
+        def _():
+            keep.wait_recv()
+            pl.semaphore_wait(taker, 1)
+            pass_on.start()
 
         @pl.when(keeper)
         def _():
-            keep.wait_recv()
+            pass_on.wait_recv()
             pl.semaphore_wait(hello, 1)
             serve.start()
 
         give.wait_recv()
         out_ref[...] = result[0]
+        pl.when(relay)(pass_on.wait_send)
         pl.when(keeper)(serve.wait_send)
 
     @pl.when(worker)
@@ -360,7 +373,7 @@
         for load in loads:
             load.start()
 
-        signal(first, barrier, {"space": space + lead, "chan": core - 1})
+        signal(first, barrier, {"space": space + halfway, "chan": core - 1})
         signal(down, barrier, {"space": space + 1})
         signal(later, barrier, {"tm": time + 1})
         signal(earlier, barrier, {"tm": time - 1})
@@ -385,7 +398,8 @@
     layers, channels, taps = conv_weights.shape
     gain = soft_gain.reshape(1, channels)
     readout = readout_weight.reshape(1, channels)
-    lead = min(LEAD, spaces - 1)
+    whole = min(LEAD[1], spaces - 1)
+    lead = min(LEAD[0], whole - 1), whole
     any_space = pl.BlockSpec(memory_space=pl.ANY)
     return pl.pallas_call(
         functools.partial(kernel, spaces, times, lead),

time: 30.9 us -> 34.2 us (1.11)
  the two profiles are of different devices: /device:TPU:88 before, /device:TPU:78 now
where the time goes in v7:
time: 34.2 us; the launch traced here: 34 us
  Pallas kernels  33.4 us (98%)
  local copies, waits for them, and re-layouts  0.61 us (2%)
    pallas_call x1, Pallas kernels, per_device(): pl.pallas_call(functools.partial(kernel, spaces, times, lead), out_shape=...  33.4 us

profile of v7, /device:TPU:78, one launch (start us, length us, event | category | flops | bytes accessed | tf_op | source)
XLA Modules:
  0.0 34.0 jit_solution(15686581447014577138)
XLA Ops:
  0.0 33.4 %shard_map.73 = f32[4,8,128]{2,1,0:T(8,128)S(1)} custom-call(s32[4,8,128]{2,1,0:T(8,128)} %ev_hbm.1, bf16[4,8,128]{2,1,0:T(8,128)(2,1)} %so_hbm.1, f32[4,64]{1,0:T(4,128)} %emb_hbm.1, f32[1,64]{1,0:T(1,128)} %bitcast.2, bf16[3,64,1728]{2,1,0:T(8,128)(2,1)} %cw_hbm.1, f32[3,64]{1,0:T(4,128)} %cb_hbm.1, f32[1,64]{1,0:T(1,128)} %bitcast.3), custom_call_target="tpu_custom_call" | custom-call | tf_op jit(solution)/shard_map/pallas_call | solution.py:404
  33.4 0.6 %copy.9 = f32[4,8,128]{2,1,0:T(8,128)} copy(f32[4,8,128]{2,1,0:T(8,128)S(1)} %shard_map.73) | data formatting | bytes 32768

commit v8 on v7

--- a/solution.py
+++ b/solution.py
@@ -10,7 +10,7 @@
 F32 = jnp.float32
 BF16 = jnp.bfloat16
 MESH = pl.DeviceIdType.MESH
-LEAD = 4, 6
+LEAD = 3, 5
 
 
 def iota(shape, dim):

time: 34.2 us -> 32.5 us (0.950)
  the two profiles are of different devices: /device:TPU:78 before, /device:TPU:86 now
where the time goes in v8:
time: 32.5 us; the launch traced here: 32.3 us
  Pallas kernels  31.7 us (98%)
  local copies, waits for them, and re-layouts  0.61 us (2%)
    pallas_call x1, Pallas kernels, per_device(): pl.pallas_call(functools.partial(kernel, spaces, times, lead), out_shape=...  31.7 us

profile of v8, /device:TPU:86, one launch (start us, length us, event | category | flops | bytes accessed | tf_op | source)
XLA Modules:
  0.0 32.3 jit_solution(11254070283894281319)
XLA Ops:
  0.0 31.7 %shard_map.73 = f32[4,8,128]{2,1,0:T(8,128)S(1)} custom-call(s32[4,8,128]{2,1,0:T(8,128)} %ev_hbm.1, bf16[4,8,128]{2,1,0:T(8,128)(2,1)} %so_hbm.1, f32[4,64]{1,0:T(4,128)} %emb_hbm.1, f32[1,64]{1,0:T(1,128)} %bitcast.2, bf16[3,64,1728]{2,1,0:T(8,128)(2,1)} %cw_hbm.1, f32[3,64]{1,0:T(4,128)} %cb_hbm.1, f32[1,64]{1,0:T(1,128)} %bitcast.3), custom_call_target="tpu_custom_call" | custom-call | tf_op jit(solution)/shard_map/pallas_call | solution.py:404
  31.7 0.6 %copy.9 = f32[4,8,128]{2,1,0:T(8,128)} copy(f32[4,8,128]{2,1,0:T(8,128)S(1)} %shard_map.73) | data formatting | bytes 32768
